TPU v7x, 128 devices: a whole 4x4x4 slice. The times are simulated.
128 devices in a mesh: section: 4 (over y_hi, core), fsdp: 32 (over z, x, y_lo).
Axes of the slice: x: 4, y: 4 (y_hi: 2, y_lo: 2; y = y_hi * 2 + y_lo), z: 4, core: 2. Of those that a mesh axis runs over, the one named last changes fastest.
Arguments:
- hidden_in: bfloat16 [4096, 4096], P('fsdp'), may hold values from -6 to 6
- out_grad: bfloat16 [4096, 4096], P('fsdp'), may hold values from -6 to 6
- fast_in: float32 [4, 4096, 1024], P('section', 'fsdp'), may hold values from -6 to 6
- fast_out: float32 [4, 1024, 4096], P('section', None, 'fsdp'), may hold values from -6 to 6
- slow_in: float32 [4, 4096, 1024], P('section', 'fsdp'), may hold values from -6 to 6
- slow_out: float32 [4, 1024, 4096], P('section', None, 'fsdp'), may hold values from -6 to 6
Outputs:
- section_out: bfloat16 [4, 4096, 4096], P('section', 'fsdp')
- input_grad: bfloat16 [4, 4096, 4096], P('section', 'fsdp')
- synced_in: float32 [4, 4096, 1024], P('section', 'fsdp')
- synced_out: float32 [4, 1024, 4096], P('section', None, 'fsdp')
All inputs are finite; a program needn't handle non-finite values.
Results may differ from a plain program's by a relative error of at most 0.014.
Values may be sent and summed in bfloat16 or wider, within the bound.
A program may use at most 896 MiB of HBM per device.

v0:
```python
import math

import jax
import jax.numpy as jnp
from jax import lax
from jax.sharding import PartitionSpec as P

epsilon = 1e-05
fast_rate = 0.5
preview_mix = 0.5


def gather_turned(arrays, axis, dims):
    turned = [jnp.moveaxis(a, dim, 0) for a, dim in zip(arrays, dims)]
    widths = [t[0].size for t in turned]
    both = jnp.concatenate([t.reshape(-1, w) for t, w in zip(turned, widths)], axis=1)
    result = lax.all_gather(both, axis, axis=0, tiled=True)
    pieces = jnp.split(result, [sum(widths[:k]) for k in range(1, len(widths))], axis=1)
    return tuple(
        (
            jnp.moveaxis(b.reshape(-1, *t.shape[1:]), 0, dim)
            for b, t, dim in zip(pieces, turned, dims)
        )
    )


def from_behind(value, axis, steps):
    count = lax.axis_size(axis)
    leading, last = (max(0, -steps), min(count, count - steps))
    return lax.ppermute(value, axis, [(source, source + steps) for source in range(leading, last)])


def contract_last(left_rows, right_rows):
    return lax.dot_general(
        left_rows, right_rows, (((1,), (1,)), ((), ())), preferred_element_type=jnp.float32
    )


def contract_first(left_rows, right_rows):
    return lax.dot_general(
        left_rows, right_rows, (((0,), (0,)), ((), ())), preferred_element_type=jnp.float32
    )


def prepare(hidden, weight_in):
    widened = hidden.astype(jnp.float32)
    inverse_rms = lax.rsqrt(jnp.mean(widened * widened, axis=-1, keepdims=True) + epsilon)
    normed = (widened * inverse_rms).astype(jnp.bfloat16)
    pre_act = jnp.dot(normed, weight_in, preferred_element_type=jnp.float32)
    activated = jax.nn.silu(pre_act).astype(jnp.bfloat16)
    return (widened, inverse_rms, normed, pre_act, activated)


def advance(hidden, weight_in, weight_out):
    widened, inverse_rms, normed, pre_act, activated = prepare(hidden, weight_in)
    return (widened + jnp.dot(activated, weight_out, preferred_element_type=jnp.float32)).astype(
        jnp.bfloat16
    )


def retreat(hidden, cot_in, weight_in, weight_out):
    widened, inverse_rms, normed, pre_act, activated = prepare(hidden, weight_in)
    act_grad = contract_last(cot_in, weight_out)
    sigmoid_vals = jax.nn.sigmoid(pre_act)
    pre_grad = (act_grad * sigmoid_vals * (1.0 + pre_act * (1.0 - sigmoid_vals))).astype(
        jnp.bfloat16
    )
    norm_grad = contract_last(pre_grad, weight_in)
    unit_rows = widened * inverse_rms
    rms_grad = inverse_rms * (
        norm_grad - unit_rows * jnp.mean(norm_grad * unit_rows, axis=-1, keepdims=True)
    )
    earlier = (cot_in.astype(jnp.float32) + rms_grad).astype(jnp.bfloat16)
    return (earlier, contract_first(normed, pre_grad), contract_first(activated, cot_in))


def shards(hidden_in, out_grad, fast_in, fast_out, slow_in, slow_out):
    sections = lax.axis_size("section")
    section_index = lax.axis_index("section")
    row_count, model_width = hidden_in.shape
    branch_units = fast_in.shape[2]
    in_scale = 1.0 / math.sqrt(model_width)
    out_scale = 1.0 / math.sqrt(branch_units)
    local_in = (fast_in[0] * in_scale).astype(jnp.bfloat16)
    local_out = (fast_out[0] * out_scale).astype(jnp.bfloat16)
    weight_in, weight_out = gather_turned((local_in, local_out), "fsdp", (0, 1))
    portions = 1
    block_rows = row_count // portions
    turn_count = sections + portions - 1
    sources = hidden_in.reshape(portions, block_rows, model_width)
    targets = out_grad.reshape(portions, block_rows, model_width)
    saved_inputs = jnp.zeros_like(sources)
    produced = jnp.zeros_like(sources)
    incoming = jnp.zeros((block_rows, model_width), jnp.bfloat16)
    for timestep in range(turn_count):
        block_slot = timestep - section_index
        active = (block_slot >= 0) & (block_slot < portions)
        block_index = jnp.clip(block_slot, 0, portions - 1)
        first_input = lax.dynamic_index_in_dim(sources, block_index, 0, keepdims=False)
        section_input = jnp.where(section_index == 0, first_input, incoming)

        def run_forward():
            return advance(section_input, weight_in, weight_out)

        def skip_forward():
            return jnp.zeros_like(section_input)

        section_output = lax.cond(active, run_forward, skip_forward)
        saved_inputs = jnp.where(
            active,
            lax.dynamic_update_index_in_dim(saved_inputs, section_input, block_index, 0),
            saved_inputs,
        )
        produced = jnp.where(
            active,
            lax.dynamic_update_index_in_dim(produced, section_output, block_index, 0),
            produced,
        )
        if timestep + 1 < turn_count:
            incoming = from_behind(section_output, "section", 1)
    grad_in = jnp.zeros((model_width, branch_units), jnp.float32)
    grad_out = jnp.zeros((branch_units, model_width), jnp.float32)
    cotangents = jnp.zeros_like(sources)
    incoming = jnp.zeros((block_rows, model_width), jnp.bfloat16)
    for timestep in range(turn_count):
        block_slot = timestep - (sections - 1 - section_index)
        active = (block_slot >= 0) & (block_slot < portions)
        block_index = jnp.clip(block_slot, 0, portions - 1)
        last_cot = lax.dynamic_index_in_dim(targets, block_index, 0, keepdims=False)
        cot_in = jnp.where(section_index == sections - 1, last_cot, incoming)
        hidden = lax.dynamic_index_in_dim(saved_inputs, block_index, 0, keepdims=False)

        def run_backward():
            return retreat(hidden, cot_in, weight_in, weight_out)

        def skip_backward():
            return (
                jnp.zeros_like(cot_in),
                jnp.zeros((model_width, branch_units), jnp.float32),
                jnp.zeros((branch_units, model_width), jnp.float32),
            )

        earlier, term_in, term_out = lax.cond(active, run_backward, skip_backward)
        grad_in = grad_in + term_in
        grad_out = grad_out + term_out
        cotangents = jnp.where(
            active, lax.dynamic_update_index_in_dim(cotangents, earlier, block_index, 0), cotangents
        )
        if timestep + 1 < turn_count:
            incoming = from_behind(earlier, "section", -1)
    shard_in, shard_out = (
        lax.psum_scatter(
            (grad_in * in_scale).astype(jnp.bfloat16), "fsdp", scatter_dimension=0, tiled=True
        ).astype(jnp.float32),
        lax.psum_scatter(
            (grad_out * out_scale).astype(jnp.bfloat16), "fsdp", scatter_dimension=1, tiled=True
        ).astype(jnp.float32),
    )
    fresh_in = fast_in[0] - fast_rate * shard_in
    fresh_out = fast_out[0] - fast_rate * shard_out
    synced_first = slow_in[0] + preview_mix * (fresh_in - slow_in[0])
    synced_second = slow_out[0] + preview_mix * (fresh_out - slow_out[0])
    section_out = produced.reshape(row_count, model_width)[None]
    input_grad = cotangents.reshape(row_count, model_width)[None]
    return (section_out, input_grad, synced_first[None], synced_second[None])


def solution(mesh):
    placed = (
        P("fsdp", None),
        P("fsdp", None),
        P("section", "fsdp", None),
        P("section", None, "fsdp"),
        P("section", "fsdp", None),
        P("section", None, "fsdp"),
    )
    return jax.shard_map(
        shards,
        mesh=mesh,
        in_specs=placed,
        out_specs=(
            P("section", "fsdp", None),
            P("section", "fsdp", None),
            P("section", "fsdp", None),
            P("section", None, "fsdp"),
        ),
        check_vma=False,
    )
```

profile of v0, /device:TPU:0, one launch (start us, length us, event | category | flops | bytes accessed | tf_op | source)
XLA Modules:
  0.0 1019.0 jit_solution(3030344230402729887)
XLA Ops:
  9.7 365.5 %all-gather.2.cloned.1.call-done = bf16[4096,2048]{1,0:T(8,128)(2,1)} async-done(((bf16[128,2048]{1,0:T(8,128)(2,1)}), bf16[4096,2048]{1,0:T(8,128)(2,1)}) %all-gather.2.cloned.1.call-update) | async-done | bytes 16777232 | tf_op jit(solution)/shard_map/all_gather | solution.py:17
  375.2 11.7 %slice_bitcast_fusion = (bf16[1024,4096]{0,1:T(8,128)(2,1)}, bf16[4096,1024]{1,0:T(8,128)(2,1)}) fusion(bf16[4096,2048]{1,0:T(8,128)(2,1)} %all-gather.2.cloned.1.call-done), kind=kLoop, calls=%fused_computation.146 | loop fusion | bytes 33554432 | tf_op jit(solution)/shard_map/transpose | solution.py:21
  386.9 10.2 conditional.8
  387.2 9.9 fusion
  401.9 19.2 %collective-permute-start.1 = (bf16[128,4096]{1,0:T(8,128)(2,1)S(1)}, bf16[128,4096]{1,0:T(8,128)(2,1)S(1)}, u32[]{:S(2)}, u32[]{:S(2)}) collective-permute-start(bf16[128,4096]{1,0:T(8,128)(2,1)S(1)} %get-tuple-element.275), channel_id=1, source_target_pairs={{0,32},{32,64},{64,96},{1,33},{33,65},{65,97},{2,34},{34,66},{66,9... | collective-permute-start | bytes 3145736 | tf_op jit(solution)/shard_map/ppermute | solution.py:30
  424.7 12.4 %collective-permute-start.2 = (bf16[128,4096]{1,0:T(8,128)(2,1)S(1)}, bf16[128,4096]{1,0:T(8,128)(2,1)}, u32[]{:S(2)}, u32[]{:S(2)}) collective-permute-start(bf16[128,4096]{1,0:T(8,128)(2,1)S(1)} %get-tuple-element.276), channel_id=1, source_target_pairs={{0,32},{32,64},{64,96},{1,33},{33,65},{65,97},{2,34},{34,66},{66,9... | collective-permute-start | bytes 3145736 | tf_op jit(solution)/shard_map/ppermute | solution.py:30
  439.8 16.3 %conditional.12 = (bf16[128,4096]{1,0:T(8,128)(2,1)S(1)}, f32[4096,1024]{1,0:T(8,128)}, f32[1024,4096]{0,1:T(8,128)}) conditional(s32[]{:T(128)} %convert_element_type.171, () %tuple.75, (pred[]{:T(512)}, bf16[128,4096]{1,0:T(8,128)(2,1)S(1)}, bf16[128,4096]{1,0:T(8,128)(2,1)S(1)}, bf16[128,4096]{1,0:T(8,128)(2,1)S(1)}, ...), branch_computations={%region_12.13_spmd, %region_13.16_spmd} | conditional | flops 5382078464 | bytes 128194168 | solution.py:143
  439.8 7.9 broadcast.228
  447.7 7.9 broadcast.229.clone
  457.4 29.5 %collective-permute-done.3 = bf16[128,4096]{1,0:T(8,128)(2,1)} collective-permute-done((bf16[128,4096]{1,0:T(8,128)(2,1)S(1)}, bf16[128,4096]{1,0:T(8,128)(2,1)}, u32[]{:S(2)}, u32[]{:S(2)}) %collective-permute-start.3) | collective-permute-done | bytes 1048608 | tf_op jit(solution)/shard_map/ppermute | solution.py:30
  486.9 16.2 %conditional.13 = (bf16[128,4096]{1,0:T(8,128)(2,1)S(1)}, f32[4096,1024]{1,0:T(8,128)}, f32[1024,4096]{0,1:T(8,128)}) conditional(s32[]{:T(128)} %convert_element_type.170, () %tuple.74, (pred[]{:T(512)}, bf16[128,4096]{1,0:T(8,128)(2,1)S(1)}, bf16[128,4096]{1,0:T(8,128)(2,1)}, bf16[128,4096]{1,0:T(8,128)(2,1)S(1)}, bf16[1024,4096]{0,1:T(8,128)(2,1)}, ...), branch_computations={%region_16.17_spmd, %region_17.20_spmd} | conditional | flops 5382078464 | bytes 128194168 | solution.py:143
  487.1 8.0 broadcast.234
  495.1 8.0 broadcast.235.clone
  504.5 17.3 %collective-permute-done.4 = bf16[128,4096]{1,0:T(8,128)(2,1)} collective-permute-done((bf16[128,4096]{1,0:T(8,128)(2,1)S(1)}, bf16[128,4096]{1,0:T(8,128)(2,1)}, u32[]{:S(2)}, u32[]{:S(2)}) %collective-permute-start.4) | collective-permute-done | bytes 1048608 | tf_op jit(solution)/shard_map/ppermute | solution.py:30
  521.7 17.2 %conditional.14 = (bf16[128,4096]{1,0:T(8,128)(2,1)}, f32[4096,1024]{1,0:T(8,128)}, f32[1024,4096]{0,1:T(8,128)}) conditional(s32[]{:T(128)} %convert_element_type.169, () %tuple.73, (pred[]{:T(512)}, bf16[128,4096]{1,0:T(8,128)(2,1)S(1)}, bf16[128,4096]{1,0:T(8,128)(2,1)}, bf16[128,4096]{1,0:T(8,128)(2,1)S(1)}, bf16[1024,4096]{0,1:T(8,128)(2,1)}, ...), branch_computations={%region_20.21_spmd, %region_21.24_spmd} | conditional | flops 5382078464 | bytes 128194168 | solution.py:143
  522.1 7.9 broadcast.240
  540.3 37.3 %collective-permute-done.5 = bf16[128,4096]{1,0:T(8,128)(2,1)} collective-permute-done((bf16[128,4096]{1,0:T(8,128)(2,1)}, bf16[128,4096]{1,0:T(8,128)(2,1)}, u32[]{:S(2)}, u32[]{:S(2)}) %collective-permute-start.5) | collective-permute-done | bytes 1048608 | tf_op jit(solution)/shard_map/ppermute | solution.py:30
  577.6 29.3 %conditional.15 = (bf16[128,4096]{1,0:T(8,128)(2,1)}, f32[4096,1024]{1,0:T(8,128)}, f32[1024,4096]{0,1:T(8,128)}) conditional(s32[]{:T(128)} %convert_element_type.168, () %tuple.72, (pred[]{:T(512)}, bf16[128,4096]{1,0:T(8,128)(2,1)S(1)}, bf16[128,4096]{1,0:T(8,128)(2,1)}, bf16[128,4096]{1,0:T(8,128)(2,1)S(1)}, bf16[1024,4096]{0,1:T(8,128)(2,1)}, ...), branch_computations={%region_24.25_spmd, %region_25.28_spmd} | conditional | flops 5382078464 | bytes 128194168 | solution.py:143
  585.8 8.2 fusion.113
  598.6 8.1 fusion.117
  606.9 26.0 %multiply_convert_fusion.12 = bf16[1024,4096]{0,1:T(8,128)(2,1)} fusion(f32[1024,4096]{0,1:T(8,128)} %get-tuple-element.235, f32[1024,4096]{0,1:T(8,128)} %get-tuple-element.234, f32[1024,4096]{0,1:T(8,128)} %get-tuple-element.232, f32[1024,4096]{0,1:T(8,128)} %get-tuple-element.233), kind=kLoop, calls=%fused_computation.144 | loop fusion | flops 20971520 | bytes 75497472 | tf_op jit(solution)/shard_map/convert_element_type | solution.py:156
  633.0 26.3 %multiply_convert_fusion.13 = bf16[4096,1024]{1,0:T(8,128)(2,1)} fusion(f32[4096,1024]{1,0:T(8,128)} %get-tuple-element.151, f32[4096,1024]{1,0:T(8,128)} %get-tuple-element.150, f32[4096,1024]{1,0:T(8,128)} %get-tuple-element.148, f32[4096,1024]{1,0:T(8,128)} %get-tuple-element.149), kind=kLoop, calls=%fused_computation.145 | loop fusion | flops 20971520 | bytes 75497472 | tf_op jit(solution)/shard_map/convert_element_type | solution.py:153
  666.2 153.1 %reduce-scatter.5.cloned.1.call-done = bf16[1024,128]{0,1:T(8,128)(2,1)} async-done(((bf16[1024,4096]{0,1:T(8,128)(2,1)}), bf16[1024,128]{0,1:T(8,128)(2,1)}) %reduce-scatter.5.cloned.1.call-update) | async-done | bytes 262160 | tf_op jit(solution)/shard_map/reduce_scatter | solution.py:155
  821.4 189.0 %reduce-scatter.3.cloned.1.call-done = bf16[128,1024]{1,0:T(8,128)(2,1)} async-done(((bf16[4096,1024]{1,0:T(8,128)(2,1)}), bf16[128,1024]{1,0:T(8,128)(2,1)}) %reduce-scatter.3.cloned.1.call-update) | async-done | bytes 262160 | tf_op jit(solution)/shard_map/reduce_scatter | solution.py:152
  (87 shorter events, 50.5 us)
Async XLA Ops:
  7.2 2.5 copy-start.1
  7.2 368.1 %all-gather.2.cloned.1.call-start = ((), (), s32[]{:S(2)}) async-start(), calls=%async_computation.2 | async-start | bytes 17301504 | tf_op jit(solution)/shard_map/all_gather | solution.py:17
  9.6 809.8 %reduce-scatter.5.cloned.1.call-start = ((), (), s32[]{:S(2)}) async-start(), calls=%async_computation.4 | async-start | bytes 8650752 | tf_op jit(solution)/shard_map/reduce_scatter | solution.py:155
  397.1 4.7 copy-start.6
  397.1 3.6 collective-permute-start
  401.8 22.5 %copy-start.7 = (bf16[128,4096]{1,0:T(8,128)(2,1)}, bf16[128,4096]{1,0:T(8,128)(2,1)S(1)}, u32[]{:S(2)}) copy-start(bf16[128,4096]{1,0:T(8,128)(2,1)S(1)} %get-tuple-element.275) | copy-start | bytes 3145732
  401.9 21.4 %collective-permute-start.1 = (bf16[128,4096]{1,0:T(8,128)(2,1)S(1)}, bf16[128,4096]{1,0:T(8,128)(2,1)S(1)}, u32[]{:S(2)}, u32[]{:S(2)}) collective-permute-start(bf16[128,4096]{1,0:T(8,128)(2,1)S(1)} %get-tuple-element.275), channel_id=1, source_target_pairs={{0,32},{32,64},{64,96},{1,33},{33,65},{65,97},{2,34},{34,66},{66,9... | collective-permute-start | bytes 3145736 | tf_op jit(solution)/shard_map/ppermute | solution.py:30
  424.7 12.4 %copy-start.8 = (bf16[128,4096]{1,0:T(8,128)(2,1)}, bf16[128,4096]{1,0:T(8,128)(2,1)S(1)}, u32[]{:S(2)}) copy-start(bf16[128,4096]{1,0:T(8,128)(2,1)S(1)} %get-tuple-element.276) | copy-start | bytes 3145732
  424.7 13.8 %collective-permute-start.2 = (bf16[128,4096]{1,0:T(8,128)(2,1)S(1)}, bf16[128,4096]{1,0:T(8,128)(2,1)}, u32[]{:S(2)}, u32[]{:S(2)}) collective-permute-start(bf16[128,4096]{1,0:T(8,128)(2,1)S(1)} %get-tuple-element.276), channel_id=1, source_target_pairs={{0,32},{32,64},{64,96},{1,33},{33,65},{65,97},{2,34},{34,66},{66,9... | collective-permute-start | bytes 3145736 | tf_op jit(solution)/shard_map/ppermute | solution.py:30
  437.1 2.7 copy-start
  456.1 30.8 %copy-start.4 = (bf16[128,4096]{1,0:T(8,128)(2,1)}, bf16[128,4096]{1,0:T(8,128)(2,1)S(1)}, u32[]{:S(2)}) copy-start(bf16[128,4096]{1,0:T(8,128)(2,1)S(1)} %get-tuple-element.144) | copy-start | bytes 3145732
  456.1 30.8 %collective-permute-start.3 = (bf16[128,4096]{1,0:T(8,128)(2,1)S(1)}, bf16[128,4096]{1,0:T(8,128)(2,1)}, u32[]{:S(2)}, u32[]{:S(2)}) collective-permute-start(bf16[128,4096]{1,0:T(8,128)(2,1)S(1)} %get-tuple-element.144), channel_id=1, source_target_pairs={{32,0},{64,32},{96,64},{33,1},{65,33},{97,65},{34,2},{66,34},{98,6... | collective-permute-start | bytes 3145736 | tf_op jit(solution)/shard_map/ppermute | solution.py:30
  503.2 18.6 %collective-permute-start.4 = (bf16[128,4096]{1,0:T(8,128)(2,1)S(1)}, bf16[128,4096]{1,0:T(8,128)(2,1)}, u32[]{:S(2)}, u32[]{:S(2)}) collective-permute-start(bf16[128,4096]{1,0:T(8,128)(2,1)S(1)} %get-tuple-element.145), channel_id=1, source_target_pairs={{32,0},{64,32},{96,64},{33,1},{65,33},{97,65},{34,2},{66,34},{98,6... | collective-permute-start | bytes 3145736 | tf_op jit(solution)/shard_map/ppermute | solution.py:30
  539.0 38.6 %collective-permute-start.5 = (bf16[128,4096]{1,0:T(8,128)(2,1)}, bf16[128,4096]{1,0:T(8,128)(2,1)}, u32[]{:S(2)}, u32[]{:S(2)}) collective-permute-start(bf16[128,4096]{1,0:T(8,128)(2,1)} %get-tuple-element.146), channel_id=1, source_target_pairs={{32,0},{64,32},{96,64},{33,1},{65,33},{97,65},{34,2},{66,34},{98,6... | collective-permute-start | bytes 3145736 | tf_op jit(solution)/shard_map/ppermute | solution.py:30
  578.1 6.2 slice-start.14
  578.1 6.2 slice-start.15
  584.3 9.7 slice-start.6
  585.8 8.2 slice-start.7
  632.9 377.5 %reduce-scatter.3.cloned.1.call-start = ((), (), s32[]{:S(2)}) async-start(), calls=%async_computation.3 | async-start | bytes 8650752 | tf_op jit(solution)/shard_map/reduce_scatter | solution.py:152
  661.3 1.6 copy-start.5
  662.9 156.5 %copy-start.3 = (f32[1,1024,128]{1,2,0:T(8,128)S(1)}, f32[1,1024,128]{1,2,0:T(8,128)}, u32[]{:S(2)}) copy-start(f32[1,1024,128]{1,2,0:T(8,128)} %copy-done.2) | copy-start | bytes 1572868
  662.9 156.5 %copy-start.12 = (f32[1,1024,128]{1,2,0:T(8,128)S(1)}, f32[1,1024,128]{1,2,0:T(8,128)}, u32[]{:S(2)}) copy-start(f32[1,1024,128]{1,2,0:T(8,128)} %copy.33) | copy-start | bytes 1572868
  666.2 344.2 %copy-start.11 = (f32[1,128,1024]{2,1,0:T(8,128)S(1)}, f32[1,128,1024]{2,1,0:T(8,128)}, u32[]{:S(2)}) copy-start(f32[1,128,1024]{2,1,0:T(8,128)} %param.24) | copy-start | bytes 1572868
  666.2 344.2 %copy-start.13 = (f32[1,128,1024]{2,1,0:T(8,128)S(1)}, f32[1,128,1024]{2,1,0:T(8,128)}, u32[]{:S(2)}) copy-start(f32[1,128,1024]{2,1,0:T(8,128)} %param.26) | copy-start | bytes 1572868
  (4 other events, 4.6 us)
Sparse Core Ops, SparseCore 0:
  10.2 364.9 all-gather.1
  633.0 186.2 reduce-scatter.4
  821.8 188.5 reduce-scatter.2
where the time goes:
time: 1030 us; the launch traced here: 1020 us
  waiting for transfers between devices  798 us (77%)
  local copies, waits for them, and re-layouts  66.7 us (6%)
  other arithmetic  66.4 us (6%)
  starting transfers between devices  36.9 us (4%)
  matrix products  35.5 us (3%)
  between operations  14.3 us (1%)
    all_gather x1, waiting for transfers between devices, gather_turned(): result = lax.all_gather(both, axis, axis=0, tiled=True)  366 us
    reduce_scatter x1, waiting for transfers between devices, shards(): lax.psum_scatter((grad_in * in_scale).astype(jnp.bfloat16), 'fsdp', scatt...  189 us
    reduce_scatter x1, waiting for transfers between devices, shards(): lax.psum_scatter((grad_out * out_scale).astype(jnp.bfloat16), 'fsdp', sca...  153 us
    ppermute x6, waiting for transfers between devices, from_behind(): lax.ppermute(value, axis, [(source, source + steps) for source in range(l...  89.9 us
    another operation x13, local copies, waits for them, and re-layouts  49.1 us
    ppermute x6, starting transfers between devices, from_behind(): lax.ppermute(value, axis, [(source, source + steps) for source in range(l...  36.8 us
    convert_element_type x1, other arithmetic, shards(): (grad_in * in_scale).astype(jnp.bfloat16)  26.3 us
    convert_element_type x1, other arithmetic, shards(): (grad_out * out_scale).astype(jnp.bfloat16)  26 us
  transfers between devices with their start and end apart: 9, of which 9 were waited for; matrix products, arithmetic and copies ran while one was open for 3% of the time, Pallas kernels for 0%

commit v1 on v0

v1 whole, which is shorter than its diff:
```python
import functools
import math

import jax
import jax.numpy as jnp
from jax import lax
from jax.experimental import pallas as pl
from jax.experimental.pallas import tpu as pltpu
from jax.sharding import PartitionSpec as P

EPS = 1e-05
RATE = 0.5
MIX = 0.5
MESH = pl.DeviceIdType.MESH
BF = jnp.bfloat16
F32 = jnp.float32
EXT = 128


def split_lanes(column):
    high = column.astype(BF)
    low = (column - high.astype(F32)).astype(BF)
    lane = lax.broadcasted_iota(jnp.int32, (column.shape[0], EXT), 1)
    return jnp.where(lane < EXT // 2, high.astype(F32), low.astype(F32)).astype(BF)


def join_lanes(lanes):
    return jnp.sum(lanes.astype(F32), axis=-1, keepdims=True) * (2.0 / EXT)


def relay(
    hid_hbm, cot_hbm, fin_hbm, fout_hbm,
    so_hbm, ig_hbm, gw_ref,
    fin, fout, hid, cot, stage0, W, G, Gx, h, g, stg, land, act, pgb, pre, rinv,
    z1, z2, za, zb, gw,
    in_sem, s_send, s_recv,
):
    D, LAT = 4096, 1024
    in_scale, out_scale = 1.0 / math.sqrt(D), 1.0 / math.sqrt(LAT)
    s = lax.axis_index("section")
    f = lax.axis_index("fsdp")
    core, yh = s % 2, s // 2
    z, x, yl = f // 8, (f // 2) % 4, f % 2
    y = yh * 2 + yl
    other = 1 - core

    def dev(yy, zz, xx, cc):
        return ((yy // 2) * 2 + cc, zz * 8 + xx * 2 + yy % 2)

    counters = {"s": 0, "r": 0}
    sends = []

    def sem(kind, n=1):
        at = counters[kind]
        counters[kind] += n
        return at

    def push(src, dst, recv_index, to):
        copy = pltpu.make_async_remote_copy(
            src_ref=src, dst_ref=dst, send_sem=s_send.at[sem("s")], recv_sem=s_recv.at[recv_index],
            device_id=to, device_id_type=MESH,
        )
        copy.start()
        sends.append(copy)

    def got(dst, recv_index):
        pltpu.make_async_remote_copy(
            src_ref=dst, dst_ref=dst, send_sem=s_send.at[0], recv_sem=s_recv.at[recv_index],
            device_id=(s, f), device_id_type=MESH,
        ).wait_recv()

    rows = pl.ds(pl.multiple_of(s * 32, 32), 32)
    loads = [
        pltpu.make_async_copy(fin_hbm.at[0], fin, in_sem.at[0]),
        pltpu.make_async_copy(fout_hbm.at[0], fout, in_sem.at[1]),
        pltpu.make_async_copy(hid_hbm.at[rows], hid, in_sem.at[2]),
        pltpu.make_async_copy(cot_hbm.at[rows], cot, in_sem.at[3]),
    ]
    for c in loads:
        c.start()

    yp, ym, zp, zm = (y + 1) % 4, (y + 3) % 4, (z + 1) % 4, (z + 3) % 4
    to_yp, to_ym = dev(yp, z, x, core), dev(ym, z, x, core)
    to_zp, to_zm = dev(y, zp, x, core), dev(y, zm, x, core)
    partner = dev(y, z, x, other)
    barrier = pltpu.get_barrier_semaphore()
    greeted = [to_yp, to_ym, to_zp, to_zm]
    for ds in range(4):
        for dx in range(4):
            if ds or dx:
                greeted.append(((s + ds) % 4, z * 8 + ((x + dx) % 4) * 2 + yl))
    for to in greeted:
        pl.semaphore_signal(barrier, inc=1, device_id=to, device_id_type=MESH)
    pl.semaphore_wait(barrier, len(greeted))

    def xdev(d):
        return (s, z * 8 + ((x + d) % 4) * 2 + yl)

    loads[0].wait()
    W[yh, core, 0, z, yl] = (fin[...] * in_scale).astype(BF)
    loads[1].wait()
    W[yh, core, 1, z, yl] = (fout[...] * out_scale).T.astype(BF)
    own_recv = sem("r", 2)
    for k in range(2):
        ref = W.at[yh, core, k, z, yl]
        push(ref, ref, own_recv + k, partner)

    def spread(source, target, load):
        load.wait()
        base = sem("r", 4)
        slot = 0 if target is h else 1
        for xx in range(4):
            for zz in range(4):
                stage0[slot, xx, :, zz * 256:(zz + 1) * 256] = source[:, zz * 1024 + xx * 256: zz * 1024 + (xx + 1) * 256]
        level = 0 if target is h else 4
        target[level, x] = stage0[slot, x]
        for d in (1, 3, 2):
            push(stage0.at[slot, (x + d) % 4], target.at[level, x], base + d, xdev(d))
        return base

    def ag_ring(item, half, q, to_plus, to_minus):
        base = sem("r", 8)
        qp, qm, qo = (q + 1) % 4, (q + 3) % 4, (q + 2) % 4
        push(item(q), item(q), base + 0, to_plus)
        push(item(q), item(q), base + 1, to_minus)
        yield
        got(item(qm), base + 0)
        push(half(qm, 0), half(qm, 0), base + 2, to_plus)
        push(item(qm), item(qm), base + 4, partner)
        yield
        got(item(qp), base + 1)
        push(half(qp, 1), half(qp, 1), base + 3, to_minus)
        push(item(qp), item(qp), base + 5, partner)
        yield
        got(half(qo, 0), base + 2)
        push(half(qo, 0), half(qo, 0), base + 6, partner)
        yield
        got(half(qo, 1), base + 3)
        push(half(qo, 1), half(qo, 1), base + 7, partner)
        pending.append(lambda: twin(item, half, q, base))

    pending = []

    def twin(item, half, q, base):
        qp, qm, qo = (q + 1) % 4, (q + 3) % 4, (q + 2) % 4
        got(item(qm, other), base + 4)
        got(item(qp, other), base + 5)
        got(half(qo, 0, other), base + 6)
        got(half(qo, 1, other), base + 7)

    def ag_round(r):
        def item_a1(c, k=core):
            return W.at[c // 2, r, k, z, c % 2, 0:64]

        def half_a1(c, n, k=core):
            return W.at[c // 2, r, k, z, c % 2, 32 * n:32 * n + 32]

        def item_b1(c, k=core):
            return W.at[yh, r, k, c, yl, 64:128]

        def half_b1(c, n, k=core):
            return W.at[yh, r, k, c, yl, 64 + 32 * n:96 + 32 * n]

        def item_a2(c, k=core):
            return W.at[:, r, k, c, :, 0:64]

        def half_a2(c, n, k=core):
            return W.at[n, r, k, c, :, 0:64]

        def item_b2(c, k=core):
            return W.at[c // 2, r, k, :, c % 2, 64:128]

        def half_b2(c, n, k=core):
            return W.at[c // 2, r, k, 2 * n:2 * n + 2, c % 2, 64:128]

        first = [ag_ring(item_a1, half_a1, y, to_yp, to_ym), ag_ring(item_b1, half_b1, z, to_zp, to_zm)]
        yield from zipped(first)
        second = [ag_ring(item_a2, half_a2, z, to_zp, to_zm), ag_ring(item_b2, half_b2, y, to_yp, to_ym)]
        yield from zipped(second)

    def zipped(tasks):
        tasks = list(tasks)
        while tasks:
            for t in list(tasks):
                try:
                    next(t)
                except StopIteration:
                    tasks.remove(t)
            yield

    def drain(task):
        for _ in task:
            pass

    def wtile(l, k, c0, n):
        return W[l // 2, l % 2, k, :, :, :, c0:c0 + n].reshape(1024, n)

    def dot_nn(a, b):
        return lax.dot_general(a, b, (((1,), (0,)), ((), ())), preferred_element_type=F32)

    def dot_nt(a, b):
        return lax.dot_general(a, b, (((1,), (1,)), ((), ())), preferred_element_type=F32)

    def dot_tn(a, b):
        return lax.dot_general(a, b, (((0,), (0,)), ((), ())), preferred_element_type=F32)

    NT = 256

    def project(source, level, l, k, step):
        left = source[level].reshape(128, 1024)

        def body(i, carry):
            c = pl.multiple_of(i * NT, NT)
            right = W[l // 2, l % 2, k, :, :, :, pl.ds(c, NT)].reshape(1024, NT)
            stg[step, :, :, pl.ds(c, NT)] = dot_nn(left, right).astype(BF).reshape(4, 32, NT)
            return carry
        lax.fori_loop(0, LAT // NT, body, 0)

    def scatter(step):
        base = sem("r", 4)
        land[step, x] = stg[step, x]
        for d in (2, 1, 3):
            push(stg.at[step, (x + d) % 4], land.at[step, x], base + d, xdev(d))
        return base

    def summed(step, base):
        for d in (1, 3, 2):
            got(land.at[step, (x + 4 - d) % 4], base + d)

    def broadcast(buf, l):
        base = sem("r", 4)
        for d in (2, 1, 3):
            push(buf.at[l, x], buf.at[l, x], base + d, xdev(d))
        return base

    def collect(buf, l, base):
        for d in (1, 3, 2):
            got(buf.at[l, (x + 4 - d) % 4], base + d)

    def emit(source, level, l, out_ref):
        base = sem("r", 16)
        mine = s * 4 + x
        for d in range(4):
            src = source.at[level, (x + d) % 4]
            dst = out_ref.at[x, rows]
            to = (l, z * 8 + ((x + d) % 4) * 2 + yl)
            copy = pltpu.make_async_remote_copy(
                src_ref=src, dst_ref=dst, send_sem=s_send.at[sem("s")], recv_sem=s_recv.at[base + mine],
                device_id=to, device_id_type=MESH,
            )
            if d:
                copy.start()
                sends.append(copy)
            else:
                local = pltpu.make_async_copy(src, dst, in_sem.at[4 + sem("l")])

                @pl.when(s != l)
                def _():
                    copy.start()

                @pl.when(s == l)
                def _():
                    local.start()
                locals_.append((l, copy, local))
        emitted.append((l, base, out_ref))

    counters["l"] = 0
    locals_, emitted = [], []

    def finish_emit():
        for l, copy, local in locals_:
            @pl.when(s != l)
            def _():
                copy.wait_send()

            @pl.when(s == l)
            def _():
                local.wait()
        for l, base, out_ref in emitted:
            @pl.when(s == l)
            def _():
                for ds in range(4):
                    for dx in range(4):
                        if ds or dx:
                            ss, xx = (s + ds) % 4, (x + dx) % 4
                            got(out_ref.at[xx, pl.ds(pl.multiple_of(ss * 32, 32), 32)], base + ss * 4 + xx)

    def forward(l):
        project(h, l, l, 0, l)
        wide = h[l].reshape(128, 1024).astype(F32)
        ss = jnp.sum(wide * wide, axis=-1, keepdims=True)
        stg[l, :, :, LAT:] = split_lanes(ss).reshape(4, 32, EXT)
        base = scatter(l)
        yield
        summed(l, base)
        total = land[l, 0].astype(F32)
        for xx in range(1, 4):
            total = total + land[l, xx].astype(F32)
        r = lax.rsqrt(join_lanes(total[:, LAT:]) * (1.0 / D) + EPS)
        v = total[:, :LAT] * r
        pre[l] = v
        rinv[l] = jnp.broadcast_to(r, (32, EXT))
        act[l, x] = (v / (1.0 + jnp.exp(-v))).astype(BF)
        base = broadcast(act, l)
        yield
        collect(act, l, base)
        left = act[l].reshape(128, 1024)

        def body(i, carry):
            c = pl.multiple_of(i * NT, NT)
            right = W[l // 2, l % 2, 1, i].reshape(NT, 1024)
            old = h[l, :, :, pl.ds(c, NT)].reshape(128, NT).astype(F32)
            h[l + 1, :, :, pl.ds(c, NT)] = (old + dot_nt(left, right)).astype(BF).reshape(4, 32, NT)
            return carry
        lax.fori_loop(0, 4, body, 0)
        emit(h, l + 1, l, so_hbm)

    def wgrad(l, kind, left_ref, left_level, right_ref, scale):
        right = right_ref[l, :, :, :LAT].reshape(128, LAT)

        def body(i, carry):
            c = pl.multiple_of(i * 128, 128)
            left = left_ref[left_level, :, :, pl.ds(c, 128)].reshape(128, 128)
            value = (dot_tn(left, right) * scale).astype(BF)
            G[l // 2, l % 2, kind, i // 2, i % 2] = value
            return carry
        lax.fori_loop(0, 8, body, 0)

    def backward(l):
        step = 7 - l
        project(g, l + 1, l, 1, step)
        base = scatter(step)
        yield
        wgrad(l, 1, g, l + 1, act, out_scale)
        summed(step, base)
        total = land[step, 0, :, :LAT].astype(F32)
        for xx in range(1, 4):
            total = total + land[step, xx, :, :LAT].astype(F32)
        v = pre[l]
        r = rinv[l][:, :1]
        sg = 1.0 / (1.0 + jnp.exp(-v))
        scaled = (r * (total * sg * (1.0 + v * (1.0 - sg)))).astype(BF)
        kappa = r * jnp.sum(scaled.astype(F32) * v, axis=-1, keepdims=True) * (1.0 / D)
        pgb[l, x, :, :LAT] = scaled
        pgb[l, x, :, LAT:] = split_lanes(kappa)
        base = broadcast(pgb, l)
        yield
        collect(pgb, l, base)
        left = pgb[l, :, :, :LAT].reshape(128, LAT)
        kap = join_lanes(pgb[l, :, :, LAT:].reshape(128, EXT))

        def body(i, carry):
            c = pl.multiple_of(i * NT, NT)
            right = W[l // 2, l % 2, 0, i].reshape(NT, 1024)
            old = g[l + 1, :, :, pl.ds(c, NT)].reshape(128, NT).astype(F32)
            base_h = h[l, :, :, pl.ds(c, NT)].reshape(128, NT).astype(F32)
            g[l, :, :, pl.ds(c, NT)] = (old + dot_nt(left, right) - base_h * kap).astype(BF).reshape(4, 32, NT)
            return carry
        lax.fori_loop(0, 4, body, 0)
        emit(g, l, l, ig_hbm)
        wgrad(l, 0, h, l, pgb, in_scale)
        gx_base[l] = sem("r")
        push(G.at[l // 2, l % 2, other], Gx.at[l // 2, l % 2], gx_base[l], partner)

    gx_base = {}

    def merge(l):
        got(Gx.at[l // 2, l % 2], gx_base[l])

        def body(i, carry):
            G[l // 2, l % 2, core, i // 2, i % 2] = G[l // 2, l % 2, core, i // 2, i % 2] + Gx[l // 2, l % 2, i // 2, i % 2]
            return carry
        lax.fori_loop(0, 8, body, 0)

    def rs_ring(half, lands, q, to_plus, to_minus, parts, result):
        p1, m1, p2, m2 = lands
        base = sem("r", 6)
        qp, qm, qo = (q + 1) % 4, (q + 3) % 4, (q + 2) % 4
        push(half(qo, 0), p1, base + 0, to_plus)
        push(half(qo, 1), m1, base + 1, to_minus)
        push(half(qp, 1), p2(1), base + 2, to_plus)
        push(half(qm, 0), m2(0), base + 3, to_minus)
        yield
        got(p1, base + 0)
        parts(half(qp, 0), half(qp, 0), [p1])
        push(half(qp, 0), p2(0), base + 4, to_plus)
        yield
        got(m1, base + 1)
        parts(half(qm, 1), half(qm, 1), [m1])
        push(half(qm, 1), m2(1), base + 5, to_minus)
        yield
        got(m2(0), base + 3)
        got(p2(1), base + 2)
        got(p2(0), base + 4)
        parts(half(q, 0), result(0), [p2(0), m2(0)])
        yield
        got(m2(1), base + 5)
        parts(half(q, 1), result(1), [p2(1), m2(1)])

    def add_flat(shape):
        count = math.prod(shape)

        def run(own, out, terms):
            def body(i, carry):
                index, rest = [], i
                for n in reversed(shape):
                    index.insert(0, rest % n)
                    rest = rest // n
                index = tuple(index)
                value = own[index] if index else own[...]
                value = value.astype(F32)
                for t in terms:
                    value = value + (t[index] if index else t[...]).astype(F32)
                if index:
                    out[index] = value.astype(BF)
                else:
                    out[...] = value.astype(BF)
                return carry
            lax.fori_loop(0, count, body, 0)
        return run

    def rs_round(r):
        def half_a1(c, n):
            return G.at[n, r, core, c, :, 0:64]

        def half_b1(c, n):
            return G.at[c // 2, r, core, 2 * n:2 * n + 2, c % 2, 64:128]

        a1 = (z1.at[r, 0, 0], z1.at[r, 0, 1], lambda n: z2.at[r, 0, 0, n], lambda n: z2.at[r, 0, 1, n])
        b1 = (z1.at[r, 1, 0], z1.at[r, 1, 1], lambda n: z2.at[r, 1, 0, n], lambda n: z2.at[r, 1, 1, n])
        yield from zipped([
            rs_ring(half_a1, a1, z, to_zp, to_zm, add_flat((2,)), lambda n: half_a1(z, n)),
            rs_ring(half_b1, b1, y, to_yp, to_ym, add_flat((2,)), lambda n: half_b1(y, n)),
        ])

        def half_a2(c, n):
            return G.at[c // 2, r, core, z, c % 2, 32 * n:32 * n + 32]

        def half_b2(c, n):
            return G.at[yh, r, core, c, yl, 64 + 32 * n:96 + 32 * n]

        a2 = (za.at[0, r, 0], za.at[0, r, 1], lambda n: zb.at[0, r, 0, n], lambda n: zb.at[0, r, 1, n])
        b2 = (za.at[1, r, 0], za.at[1, r, 1], lambda n: zb.at[1, r, 0, n], lambda n: zb.at[1, r, 1, n])
        yield from zipped([
            rs_ring(half_a2, a2, y, to_yp, to_ym, add_flat(()), lambda n: half_a2(y, n)),
            rs_ring(half_b2, b2, z, to_zp, to_zm, add_flat(()), lambda n: half_b2(z, n)),
        ])

    hbase = spread(hid, h, loads[2])
    gbase = spread(cot, g, loads[3])
    got(W.at[yh, other, 0, z, yl], own_recv)
    got(W.at[yh, other, 1, z, yl], own_recv + 1)

    def step(task):
        next(task, None)

    def settle():
        for wait in pending:
            wait()
        pending.clear()

    drain(ag_round(0))
    late = ag_round(1)
    step(late)
    settle()
    for d in (1, 3, 2):
        got(h.at[0, (x + 4 - d) % 4], hbase + d)
    fw = forward(0)
    for _ in fw:
        step(late)
    drain(late)
    settle()
    for l in range(1, 4):
        drain(forward(l))
    for d in (1, 3, 2):
        got(g.at[4, (x + 4 - d) % 4], gbase + d)
    for l in (3, 2, 1):
        drain(backward(l))
    merge(3)
    merge(1)
    early = rs_round(1)
    step(early)
    for _ in backward(0):
        step(early)
    drain(early)
    merge(2)
    merge(0)
    drain(rs_round(0))
    last = sem("r")
    push(G.at[yh, other, core, z, yl], gw.at[core], last, partner)
    gw_ref[core] = G[yh, core, core, z, yl]
    got(gw.at[other], last)
    gw_ref[other] = gw[other]
    for copy in sends:
        copy.wait_send()
    finish_emit()
    assert counters["s"] <= SENDS and counters["r"] <= RECVS and counters["l"] <= 8, counters


SENDS, RECVS = 256, 384


def shards(hidden_in, out_grad, fast_in, fast_out, slow_in, slow_out):
    any_ = pl.BlockSpec(memory_space=pl.ANY)
    so, ig, gw = pl.pallas_call(
        relay,
        out_shape=(
            jax.ShapeDtypeStruct((4, 128, 1024), BF),
            jax.ShapeDtypeStruct((4, 128, 1024), BF),
            jax.ShapeDtypeStruct((2, 128, 1024), BF),
        ),
        in_specs=[any_] * 4,
        out_specs=(any_, any_, pl.BlockSpec(memory_space=pltpu.VMEM)),
        scratch_shapes=[
            pltpu.VMEM((128, 1024), F32),
            pltpu.VMEM((1024, 128), F32),
            pltpu.VMEM((32, 4096), BF),
            pltpu.VMEM((32, 4096), BF),
            pltpu.VMEM((2, 4, 32, 1024), BF),
            pltpu.VMEM((2, 2, 2, 4, 2, 128, 1024), BF),
            pltpu.VMEM((2, 2, 2, 4, 2, 128, 1024), BF),
            pltpu.VMEM((2, 2, 4, 2, 128, 1024), BF),
            pltpu.VMEM((5, 4, 32, 1024), BF),
            pltpu.VMEM((5, 4, 32, 1024), BF),
            pltpu.VMEM((8, 4, 32, 1024 + EXT), BF),
            pltpu.VMEM((8, 4, 32, 1024 + EXT), BF),
            pltpu.VMEM((4, 4, 32, 1024), BF),
            pltpu.VMEM((4, 4, 32, 1024 + EXT), BF),
            pltpu.VMEM((4, 32, 1024), F32),
            pltpu.VMEM((4, 32, EXT), F32),
            pltpu.VMEM((2, 2, 2, 2, 64, 1024), BF),
            pltpu.VMEM((2, 2, 2, 2, 2, 64, 1024), BF),
            pltpu.VMEM((2, 2, 2, 32, 1024), BF),
            pltpu.VMEM((2, 2, 2, 2, 32, 1024), BF),
            pltpu.VMEM((2, 128, 1024), BF),
            pltpu.SemaphoreType.DMA((12,)),
            pltpu.SemaphoreType.DMA((SENDS,)),
            pltpu.SemaphoreType.DMA((RECVS,)),
        ],
        compiler_params=pltpu.CompilerParams(
            collective_id=0, has_side_effects=True, vmem_limit_bytes=67043328
        ),
        name="relay",
    )(hidden_in, out_grad, fast_in, fast_out)

    def whole(pieces):
        return pieces.reshape(4, 128, 4, 256).transpose(1, 2, 0, 3).reshape(1, 128, 4096)

    def synced(fast, slow, grad):
        fresh = fast - RATE * grad
        return slow + MIX * (fresh - slow)

    grad_in = gw[0].astype(F32)
    grad_out = gw[1].astype(F32).T
    return (
        whole(so), whole(ig),
        synced(fast_in, slow_in, grad_in[None]),
        synced(fast_out, slow_out, grad_out[None]),
    )


def solution(mesh):
    placed = (
        P("fsdp", None), P("fsdp", None),
        P("section", "fsdp", None), P("section", None, "fsdp"),
        P("section", "fsdp", None), P("section", None, "fsdp"),
    )
    return jax.shard_map(
        shards, mesh=mesh, in_specs=placed,
        out_specs=(
            P("section", "fsdp", None), P("section", "fsdp", None),
            P("section", "fsdp", None), P("section", None, "fsdp"),
        ),
        check_vma=False,
    )
```

time: 1030 us -> 254 us (0.25)
  waiting for transfers between devices: 798 us -> 0 us
  Pallas kernels: 0 us -> 236 us
  other arithmetic: 66.4 us -> 3.42 us
  local copies, waits for them, and re-layouts: 66.7 us -> 11.6 us
  starting transfers between devices: 36.9 us -> 0 us
  matrix products: 35.5 us -> 0 us
  between operations: 14.3 us -> 0.71 us
    all_gather x1 -> x0, waiting for transfers between devices: 366 us -> none  [gather_turned(): result = lax.all_gather(both, axis, axis=0, tiled=True)]
    reduce_scatter x2 -> x0, waiting for transfers between devices: 342 us -> none  [the longest x1 189 us: shards(): lax.psum_scatter((grad_in * in_scale).astype(jnp.bfloat16), 'fsdp', scatt...]
    pallas_call x0 -> x1, Pallas kernels: none -> 236 us  [shards(): pl.pallas_call(relay, out_shape=(jax.ShapeDtypeStruct((4, 128, 1024), BF)...]
    ppermute x6 -> x0, waiting for transfers between devices: 89.9 us -> none  [from_behind(): lax.ppermute(value, axis, [(source, source + steps) for source in range(l...]
    convert_element_type x4 -> x0, other arithmetic: 53.9 us -> none  [the longest x1 26.3 us: shards(): (grad_in * in_scale).astype(jnp.bfloat16)]
    another operation x13 -> x0, local copies, waits for them, and re-layouts: 49.1 us -> none
    ppermute x6 -> x0, starting transfers between devices: 36.8 us -> none  [from_behind(): lax.ppermute(value, axis, [(source, source + steps) for source in range(l...]
    dot_general x5 -> x0, matrix products: 27.3 us -> none  [the longest x1 9.87 us: advance(): jnp.dot(activated, weight_out, preferred_element_type=jnp.float32)]
  transfers between devices with their start and end apart: 9 -> 0, of which waited for: 9 -> 0; matrix products, arithmetic and copies ran while one was open for 3% -> 0% of each run, Pallas kernels for 0% -> 0%
where the time goes in v1:
time: 254 us; the launch traced here: 252 us
  Pallas kernels  236 us (93%)
  local copies, waits for them, and re-layouts  11.6 us (5%)
  other arithmetic  3.42 us (1%)
    pallas_call x1, Pallas kernels, shards(): pl.pallas_call(relay, out_shape=(jax.ShapeDtypeStruct((4, 128, 1024), BF)...  236 us

profile of v1, /device:TPU:0, one launch (start us, length us, event | category | flops | bytes accessed | tf_op | source)
XLA Modules:
  0.0 252.1 jit_solution(11944316055204616945)
XLA Ops:
  0.6 0.0 copy-start.1
  0.6 2.1 copy.14
  2.7 0.0 copy-done.1
  2.7 1.0 copy.12
  3.7 236.4 %relay.1 = (bf16[4,128,1024]{2,1,0:T(8,128)(2,1)}, bf16[4,128,1024]{2,1,0:T(8,128)(2,1)}, bf16[2,128,1024]{2,1,0:T(8,128)(2,1)}) custom-call(bf16[128,4096]{1,0:T(8,128)(2,1)} %hid_hbm.1, bf16[128,4096]{1,0:T(8,128)(2,1)} %cot_hbm.1, f32[1,128,1024]{2,1,0:T(8,128)} %fin_hbm.1, f32[1,1024,128]{2,1,0:T(8,128)} %fout_hbm.1), custom_call_target="tpu_custom_call" | custom-call | tf_op jit(solution)/shard_map/relay/pallas_call | solution.py:505
  240.1 0.0 copy-start.3
  240.1 1.5 fusion.2
  241.6 1.0 copy.15
  242.6 0.0 copy-done.3
  242.6 0.8 reshape.25
  243.4 1.4 copy.10
  244.7 0.0 copy-start
  244.8 0.0 copy-start.4
  244.8 1.6 reshape.26
  246.4 0.0 copy-done
  246.4 0.0 copy-done.4
  246.4 0.0 copy-start.2
  246.4 1.9 multiply_add_fusion
  248.3 0.0 copy-done.2
  248.3 0.8 reshape.27
  249.1 1.4 copy.11
  250.5 1.6 reshape.28
Async XLA Ops:
  0.6 2.1 copy-start.1
  240.1 2.5 copy-start.3
  244.7 1.6 copy-start
  244.8 1.6 copy-start.4
  246.4 2.0 copy-start.2

commit v2 on v1

--- a/solution.py
+++ b/solution.py
@@ -31,7 +31,7 @@
 def relay(
     hid_hbm, cot_hbm, fin_hbm, fout_hbm,
     so_hbm, ig_hbm, gw_ref,
-    fin, fout, hid, cot, stage0, W, G, Gx, h, g, stg, land, act, pgb, pre, rinv,
+    fin, fout, hid, cot, stage0, own, W, G, Gx, h, g, stg, land, act, pgb, pre, rinv,
     z1, z2, za, zb, gw,
     in_sem, s_send, s_recv,
 ):
@@ -96,14 +96,29 @@
     def xdev(d):
         return (s, z * 8 + ((x + d) % 4) * 2 + yl)
 
-    loads[0].wait()
-    W[yh, core, 0, z, yl] = (fin[...] * in_scale).astype(BF)
-    loads[1].wait()
-    W[yh, core, 1, z, yl] = (fout[...] * out_scale).T.astype(BF)
-    own_recv = sem("r", 2)
-    for k in range(2):
-        ref = W.at[yh, core, k, z, yl]
-        push(ref, ref, own_recv + k, partner)
+    def quarters(rows):
+        return rows.astype(BF).reshape(2, 2, 32, LAT)
+
+    mates = sem("r", 8)
+
+    def share():
+        loads[0].wait()
+        own[0] = quarters(fin[...] * in_scale)
+        loads[1].wait()
+        own[1] = quarters((fout[...] * out_scale).T)
+        for c in range(2):
+            push(own.at[c, 1 - yh], W.at[s, c, z, yl, 1 - yh], mates + core, ((1 - yh) * 2 + c, f))
+        push(own.at[:, yh], W.at[s, :, z, yl, yh], mates + 2, partner)
+        W[s, 0, z, yl, yh] = own[0, yh]
+        W[s, 1, z, yl, yh] = own[1, yh]
+
+    def shared():
+        far = pl.ds(2 * (1 - yh), 2)
+        for c in range(2):
+            got(W.at[2 * (1 - yh) + c, core, z, yl, yh], mates + c)
+        push(W.at[far, core, z, yl, yh], W.at[far, core, z, yl, yh], mates + 3, partner)
+        got(W.at[yh * 2 + other, :, z, yl, yh], mates + 2)
+        pending.append((0, lambda: got(W.at[far, other, z, yl, yh], mates + 3)))
 
     def spread(source, target, load):
         load.wait()
@@ -118,7 +133,7 @@
             push(stage0.at[slot, (x + d) % 4], target.at[level, x], base + d, xdev(d))
         return base
 
-    def ag_ring(item, half, q, to_plus, to_minus):
+    def ag_ring(item, half, q, to_plus, to_minus, level):
         base = sem("r", 8)
         qp, qm, qo = (q + 1) % 4, (q + 3) % 4, (q + 2) % 4
         push(item(q), item(q), base + 0, to_plus)
@@ -126,18 +141,16 @@
         yield
         got(item(qm), base + 0)
         push(half(qm, 0), half(qm, 0), base + 2, to_plus)
-        push(item(qm), item(qm), base + 4, partner)
-        yield
         got(item(qp), base + 1)
         push(half(qp, 1), half(qp, 1), base + 3, to_minus)
+        push(item(qm), item(qm), base + 4, partner)
         push(item(qp), item(qp), base + 5, partner)
         yield
         got(half(qo, 0), base + 2)
         push(half(qo, 0), half(qo, 0), base + 6, partner)
-        yield
         got(half(qo, 1), base + 3)
         push(half(qo, 1), half(qo, 1), base + 7, partner)
-        pending.append(lambda: twin(item, half, q, base))
+        pending.append((level, lambda: twin(item, half, q, base)))
 
     pending = []
 
@@ -148,53 +161,55 @@
         got(half(qo, 0, other), base + 6)
         got(half(qo, 1, other), base + 7)
 
-    def ag_round(r):
-        def item_a1(c, k=core):
-            return W.at[c // 2, r, k, z, c % 2, 0:64]
-
-        def half_a1(c, n, k=core):
-            return W.at[c // 2, r, k, z, c % 2, 32 * n:32 * n + 32]
-
-        def item_b1(c, k=core):
-            return W.at[yh, r, k, c, yl, 64:128]
-
-        def half_b1(c, n, k=core):
-            return W.at[yh, r, k, c, yl, 64 + 32 * n:96 + 32 * n]
-
-        def item_a2(c, k=core):
-            return W.at[:, r, k, c, :, 0:64]
-
-        def half_a2(c, n, k=core):
-            return W.at[n, r, k, c, :, 0:64]
-
-        def item_b2(c, k=core):
-            return W.at[c // 2, r, k, :, c % 2, 64:128]
-
-        def half_b2(c, n, k=core):
-            return W.at[c // 2, r, k, 2 * n:2 * n + 2, c % 2, 64:128]
-
-        first = [ag_ring(item_a1, half_a1, y, to_yp, to_ym), ag_ring(item_b1, half_b1, z, to_zp, to_zm)]
-        yield from zipped(first)
-        second = [ag_ring(item_a2, half_a2, z, to_zp, to_zm), ag_ring(item_b2, half_b2, y, to_yp, to_ym)]
-        yield from zipped(second)
+    def settle(level):
+        for entry in list(pending):
+            if entry[0] <= level:
+                entry[1]()
+                pending.remove(entry)
+
+    def gather_first(ls, level):
+        def item_a(c, k=core):
+            return W.at[ls, k, z, c % 2, c // 2, 0]
+
+        def half_a(c, n, k=core):
+            return W.at[ls, k, z, c % 2, c // 2, 0, 16 * n:16 * n + 16]
+
+        def item_b(c, k=core):
+            return W.at[ls, k, c, yl, yh, 1]
+
+        def half_b(c, n, k=core):
+            return W.at[ls, k, c, yl, yh, 1, 16 * n:16 * n + 16]
+
+        return zipped([
+            ag_ring(item_a, half_a, y, to_yp, to_ym, level), ag_ring(item_b, half_b, z, to_zp, to_zm, level)])
+
+    def gather_second(l):
+        def item_a(c, k=core):
+            return W.at[l, k, c, :, :, 0]
+
+        def half_a(c, n, k=core):
+            return W.at[l, k, c, n, :, 0]
+
+        def item_b(c, k=core):
+            return W.at[l, k, :, c % 2, c // 2, 1]
+
+        def half_b(c, n, k=core):
+            return W.at[l, k, 2 * n:2 * n + 2, c % 2, c // 2, 1]
+
+        return zipped([
+            ag_ring(item_a, half_a, z, to_zp, to_zm, l), ag_ring(item_b, half_b, y, to_yp, to_ym, l)])
 
     def zipped(tasks):
         tasks = list(tasks)
         while tasks:
-            for t in list(tasks):
-                try:
-                    next(t)
-                except StopIteration:
-                    tasks.remove(t)
-            yield
+            tasks = [t for t in tasks if next(t, True) is not True]
+            if tasks:
+                yield
 
     def drain(task):
         for _ in task:
             pass
 
-    def wtile(l, k, c0, n):
-        return W[l // 2, l % 2, k, :, :, :, c0:c0 + n].reshape(1024, n)
-
     def dot_nn(a, b):
         return lax.dot_general(a, b, (((1,), (0,)), ((), ())), preferred_element_type=F32)
 
@@ -211,7 +226,7 @@
 
         def body(i, carry):
             c = pl.multiple_of(i * NT, NT)
-            right = W[l // 2, l % 2, k, :, :, :, pl.ds(c, NT)].reshape(1024, NT)
+            right = W[l, k, :, :, :, :, :, pl.ds(c, NT)].reshape(1024, NT)
             stg[step, :, :, pl.ds(c, NT)] = dot_nn(left, right).astype(BF).reshape(4, 32, NT)
             return carry
         lax.fori_loop(0, LAT // NT, body, 0)
@@ -239,30 +254,39 @@
 
     def emit(source, level, l, out_ref):
         base = sem("r", 16)
-        mine = s * 4 + x
-        for d in range(4):
-            src = source.at[level, (x + d) % 4]
-            dst = out_ref.at[x, rows]
-            to = (l, z * 8 + ((x + d) % 4) * 2 + yl)
-            copy = pltpu.make_async_remote_copy(
-                src_ref=src, dst_ref=dst, send_sem=s_send.at[sem("s")], recv_sem=s_recv.at[base + mine],
-                device_id=to, device_id_type=MESH,
-            )
-            if d:
-                copy.start()
-                sends.append(copy)
-            else:
-                local = pltpu.make_async_copy(src, dst, in_sem.at[4 + sem("l")])
-
-                @pl.when(s != l)
-                def _():
+        emitted.append((l, base, out_ref))
+
+        def part(ds):
+            for d in ds:
+                src = source.at[level, (x + d) % 4]
+                dst = out_ref.at[x, rows]
+                to = (l, z * 8 + ((x + d) % 4) * 2 + yl)
+                copy = pltpu.make_async_remote_copy(
+                    src_ref=src, dst_ref=dst, send_sem=s_send.at[sem("s")], recv_sem=s_recv.at[base + s * 4 + x],
+                    device_id=to, device_id_type=MESH,
+                )
+                if d:
                     copy.start()
-
-                @pl.when(s == l)
-                def _():
-                    local.start()
-                locals_.append((l, copy, local))
-        emitted.append((l, base, out_ref))
+                    sends.append(copy)
+                else:
+                    local = pltpu.make_async_copy(src, dst, in_sem.at[4 + sem("l")])
+
+                    @pl.when(s != l)
+                    def _():
+                        copy.start()
+
+                    @pl.when(s == l)
+                    def _():
+                        local.start()
+                    locals_.append((l, copy, local))
+        parts_due.append(lambda: part((0, 2)))
+        parts_due.append(lambda: part((1, 3)))
+
+    parts_due = []
+
+    def emit_next():
+        if parts_due:
+            parts_due.pop(0)()
 
     counters["l"] = 0
     locals_, emitted = [], []
@@ -291,6 +315,7 @@
         ss = jnp.sum(wide * wide, axis=-1, keepdims=True)
         stg[l, :, :, LAT:] = split_lanes(ss).reshape(4, 32, EXT)
         base = scatter(l)
+        emit_next()
         yield
         summed(l, base)
         total = land[l, 0].astype(F32)
@@ -302,13 +327,14 @@
         rinv[l] = jnp.broadcast_to(r, (32, EXT))
         act[l, x] = (v / (1.0 + jnp.exp(-v))).astype(BF)
         base = broadcast(act, l)
+        emit_next()
         yield
         collect(act, l, base)
         left = act[l].reshape(128, 1024)
 
         def body(i, carry):
             c = pl.multiple_of(i * NT, NT)
-            right = W[l // 2, l % 2, 1, i].reshape(NT, 1024)
+            right = W[l, 1, i].reshape(NT, 1024)
             old = h[l, :, :, pl.ds(c, NT)].reshape(128, NT).astype(F32)
             h[l + 1, :, :, pl.ds(c, NT)] = (old + dot_nt(left, right)).astype(BF).reshape(4, 32, NT)
             return carry
@@ -322,7 +348,7 @@
             c = pl.multiple_of(i * 128, 128)
             left = left_ref[left_level, :, :, pl.ds(c, 128)].reshape(128, 128)
             value = (dot_tn(left, right) * scale).astype(BF)
-            G[l // 2, l % 2, kind, i // 2, i % 2] = value
+            G[l, kind, i // 2, i % 2] = value.reshape(2, 2, 32, LAT)
             return carry
         lax.fori_loop(0, 8, body, 0)
 
@@ -330,8 +356,10 @@
         step = 7 - l
         project(g, l + 1, l, 1, step)
         base = scatter(step)
-        yield
-        wgrad(l, 1, g, l + 1, act, out_scale)
+        emit_next()
+        if l < 3:
+            input_grads(l + 1)
+        yield
         summed(step, base)
         total = land[step, 0, :, :LAT].astype(F32)
         for xx in range(1, 4):
@@ -344,31 +372,39 @@
         pgb[l, x, :, :LAT] = scaled
         pgb[l, x, :, LAT:] = split_lanes(kappa)
         base = broadcast(pgb, l)
+        emit_next()
+        wgrad(l, 1, g, l + 1, act, out_scale)
         yield
         collect(pgb, l, base)
         left = pgb[l, :, :, :LAT].reshape(128, LAT)
         kap = join_lanes(pgb[l, :, :, LAT:].reshape(128, EXT))
 
+        if l == 0:
+            input_grads(0)
+
         def body(i, carry):
             c = pl.multiple_of(i * NT, NT)
-            right = W[l // 2, l % 2, 0, i].reshape(NT, 1024)
+            right = W[l, 0, i].reshape(NT, 1024)
             old = g[l + 1, :, :, pl.ds(c, NT)].reshape(128, NT).astype(F32)
             base_h = h[l, :, :, pl.ds(c, NT)].reshape(128, NT).astype(F32)
             g[l, :, :, pl.ds(c, NT)] = (old + dot_nt(left, right) - base_h * kap).astype(BF).reshape(4, 32, NT)
             return carry
         lax.fori_loop(0, 4, body, 0)
         emit(g, l, l, ig_hbm)
+
+    def input_grads(l):
         wgrad(l, 0, h, l, pgb, in_scale)
         gx_base[l] = sem("r")
-        push(G.at[l // 2, l % 2, other], Gx.at[l // 2, l % 2], gx_base[l], partner)
+        push(G.at[l, other], Gx.at[l], gx_base[l], partner)
 
     gx_base = {}
 
     def merge(l):
-        got(Gx.at[l // 2, l % 2], gx_base[l])
+        got(Gx.at[l], gx_base[l])
 
         def body(i, carry):
-            G[l // 2, l % 2, core, i // 2, i % 2] = G[l // 2, l % 2, core, i // 2, i % 2] + Gx[l // 2, l % 2, i // 2, i % 2]
+            at = (l, core, i // 2, i % 2)
+            G[at] = G[at] + Gx[l, i // 2, i % 2]
             return carry
         lax.fori_loop(0, 8, body, 0)
 
@@ -384,16 +420,14 @@
         got(p1, base + 0)
         parts(half(qp, 0), half(qp, 0), [p1])
         push(half(qp, 0), p2(0), base + 4, to_plus)
-        yield
         got(m1, base + 1)
         parts(half(qm, 1), half(qm, 1), [m1])
         push(half(qm, 1), m2(1), base + 5, to_minus)
         yield
         got(m2(0), base + 3)
-        got(p2(1), base + 2)
         got(p2(0), base + 4)
         parts(half(q, 0), result(0), [p2(0), m2(0)])
-        yield
+        got(p2(1), base + 2)
         got(m2(1), base + 5)
         parts(half(q, 1), result(1), [p2(1), m2(1)])
 
@@ -419,85 +453,127 @@
             lax.fori_loop(0, count, body, 0)
         return run
 
-    def rs_round(r):
+    def reduce_round(l):
         def half_a1(c, n):
-            return G.at[n, r, core, c, :, 0:64]
+            return G.at[l, core, c, n, :, 0]
 
         def half_b1(c, n):
-            return G.at[c // 2, r, core, 2 * n:2 * n + 2, c % 2, 64:128]
-
-        a1 = (z1.at[r, 0, 0], z1.at[r, 0, 1], lambda n: z2.at[r, 0, 0, n], lambda n: z2.at[r, 0, 1, n])
-        b1 = (z1.at[r, 1, 0], z1.at[r, 1, 1], lambda n: z2.at[r, 1, 0, n], lambda n: z2.at[r, 1, 1, n])
+            return G.at[l, core, 2 * n:2 * n + 2, c % 2, c // 2, 1]
+
+        a1 = (z1.at[l, 0, 0], z1.at[l, 0, 1], lambda n: z2.at[l, 0, 0, n], lambda n: z2.at[l, 0, 1, n])
+        b1 = (z1.at[l, 1, 0], z1.at[l, 1, 1], lambda n: z2.at[l, 1, 0, n], lambda n: z2.at[l, 1, 1, n])
         yield from zipped([
             rs_ring(half_a1, a1, z, to_zp, to_zm, add_flat((2,)), lambda n: half_a1(z, n)),
             rs_ring(half_b1, b1, y, to_yp, to_ym, add_flat((2,)), lambda n: half_b1(y, n)),
         ])
 
         def half_a2(c, n):
-            return G.at[c // 2, r, core, z, c % 2, 32 * n:32 * n + 32]
+            return G.at[l, core, z, c % 2, c // 2, 0, 16 * n:16 * n + 16]
 
         def half_b2(c, n):
-            return G.at[yh, r, core, c, yl, 64 + 32 * n:96 + 32 * n]
-
-        a2 = (za.at[0, r, 0], za.at[0, r, 1], lambda n: zb.at[0, r, 0, n], lambda n: zb.at[0, r, 1, n])
-        b2 = (za.at[1, r, 0], za.at[1, r, 1], lambda n: zb.at[1, r, 0, n], lambda n: zb.at[1, r, 1, n])
+            return G.at[l, core, c, yl, yh, 1, 16 * n:16 * n + 16]
+
+        a2 = (za.at[l, 0, 0], za.at[l, 0, 1], lambda n: zb.at[l, 0, 0, n], lambda n: zb.at[l, 0, 1, n])
+        b2 = (za.at[l, 1, 0], za.at[l, 1, 1], lambda n: zb.at[l, 1, 0, n], lambda n: zb.at[l, 1, 1, n])
         yield from zipped([
             rs_ring(half_a2, a2, y, to_yp, to_ym, add_flat(()), lambda n: half_a2(y, n)),
             rs_ring(half_b2, b2, z, to_zp, to_zm, add_flat(()), lambda n: half_b2(z, n)),
         ])
-
+        mine = G.at[l, core, z, yl, yh]
+        copy = pltpu.make_async_remote_copy(
+            src_ref=mine, dst_ref=gw.at[core, yh], send_sem=s_send.at[sem("s")], recv_sem=s_recv.at[home + s],
+            device_id=(l, f), device_id_type=MESH,
+        )
+
+        @pl.when(s != l)
+        def _():
+            copy.start()
+
+        @pl.when(s == l)
+        def _():
+            gw[core, yh] = mine[...]
+        sent_home.append((l, copy))
+
+    home = sem("r", 4)
+    sent_home = []
+
+    def step(task, n=1):
+        for _ in range(n):
+            next(task, None)
+
+    share()
     hbase = spread(hid, h, loads[2])
     gbase = spread(cot, g, loads[3])
-    got(W.at[yh, other, 0, z, yl], own_recv)
-    got(W.at[yh, other, 1, z, yl], own_recv + 1)
-
-    def step(task):
-        next(task, None)
-
-    def settle():
-        for wait in pending:
-            wait()
-        pending.clear()
-
-    drain(ag_round(0))
-    late = ag_round(1)
-    step(late)
-    settle()
+    shared()
+    ready = set()
+
+    def gather():
+        first, rest = gather_first(0, 0), gather_first(slice(1, 4), 1)
+        step(first)
+        step(rest)
+        yield
+        yield from first
+        current = gather_second(0)
+        step(current)
+        yield from rest
+        for l in range(4):
+            step(current)
+            following = gather_second(l + 1) if l < 3 else None
+            if following is not None:
+                step(following)
+            yield
+            drain(current)
+            ready.add(l)
+            yield
+            current = following
+
+    bulk = gather()
+
+    def need(l):
+        while l not in ready:
+            step(bulk)
+        settle(l)
+
+    need(0)
     for d in (1, 3, 2):
         got(h.at[0, (x + 4 - d) % 4], hbase + d)
-    fw = forward(0)
-    for _ in fw:
-        step(late)
-    drain(late)
-    settle()
-    for l in range(1, 4):
-        drain(forward(l))
+    for l in range(4):
+        need(l)
+        for _ in forward(l):
+            step(bulk)
     for d in (1, 3, 2):
         got(g.at[4, (x + 4 - d) % 4], gbase + d)
-    for l in (3, 2, 1):
-        drain(backward(l))
-    merge(3)
-    merge(1)
-    early = rs_round(1)
-    step(early)
-    for _ in backward(0):
-        step(early)
-    drain(early)
-    merge(2)
+    running = []
+    for l in (3, 2, 1, 0):
+        for n, _ in enumerate(backward(l)):
+            for task in running:
+                step(task)
+            if n == 1 and l < 3:
+                merge(l + 1)
+                running.append(reduce_round(l + 1))
+                step(running[-1])
+    while parts_due:
+        emit_next()
+    for task in running:
+        step(task)
     merge(0)
-    drain(rs_round(0))
-    last = sem("r")
-    push(G.at[yh, other, core, z, yl], gw.at[core], last, partner)
-    gw_ref[core] = G[yh, core, core, z, yl]
-    got(gw.at[other], last)
-    gw_ref[other] = gw[other]
+    running.append(reduce_round(0))
+    drain(zipped(running))
+    for l, copy in sent_home:
+        @pl.when(s != l)
+        def _():
+            copy.wait_send()
+    for ds in range(1, 4):
+        ss = (s + ds) % 4
+        got(gw.at[ss % 2, ss // 2], home + ss)
+    gw_ref[...] = gw[...].reshape(2, 128, LAT)
     for copy in sends:
         copy.wait_send()
     finish_emit()
     assert counters["s"] <= SENDS and counters["r"] <= RECVS and counters["l"] <= 8, counters
 
 
-SENDS, RECVS = 256, 384
+SENDS, RECVS = 352, 480
 
 
 def shards(hidden_in, out_grad, fast_in, fast_out, slow_in, slow_out):
@@ -517,9 +593,10 @@
             pltpu.VMEM((32, 4096), BF),
             pltpu.VMEM((32, 4096), BF),
             pltpu.VMEM((2, 4, 32, 1024), BF),
-            pltpu.VMEM((2, 2, 2, 4, 2, 128, 1024), BF),
-            pltpu.VMEM((2, 2, 2, 4, 2, 128, 1024), BF),
-            pltpu.VMEM((2, 2, 4, 2, 128, 1024), BF),
+            pltpu.VMEM((2, 2, 2, 32, 1024), BF),
+            pltpu.VMEM((4, 2, 4, 2, 2, 2, 32, 1024), BF),
+            pltpu.VMEM((4, 2, 4, 2, 2, 2, 32, 1024), BF),
+            pltpu.VMEM((4, 4, 2, 2, 2, 32, 1024), BF),
             pltpu.VMEM((5, 4, 32, 1024), BF),
             pltpu.VMEM((5, 4, 32, 1024), BF),
             pltpu.VMEM((8, 4, 32, 1024 + EXT), BF),
@@ -528,11 +605,11 @@
             pltpu.VMEM((4, 4, 32, 1024 + EXT), BF),
             pltpu.VMEM((4, 32, 1024), F32),
             pltpu.VMEM((4, 32, EXT), F32),
-            pltpu.VMEM((2, 2, 2, 2, 64, 1024), BF),
-            pltpu.VMEM((2, 2, 2, 2, 2, 64, 1024), BF),
+            pltpu.VMEM((4, 2, 2, 2, 32, 1024), BF),
+            pltpu.VMEM((4, 2, 2, 2, 2, 32, 1024), BF),
+            pltpu.VMEM((4, 2, 2, 16, 1024), BF),
+            pltpu.VMEM((4, 2, 2, 2, 16, 1024), BF),
             pltpu.VMEM((2, 2, 2, 32, 1024), BF),
-            pltpu.VMEM((2, 2, 2, 2, 32, 1024), BF),
-            pltpu.VMEM((2, 128, 1024), BF),
             pltpu.SemaphoreType.DMA((12,)),
             pltpu.SemaphoreType.DMA((SENDS,)),
             pltpu.SemaphoreType.DMA((RECVS,)),
@@ -543,20 +620,69 @@
         name="relay",
     )(hidden_in, out_grad, fast_in, fast_out)
 
-    def whole(pieces):
-        return pieces.reshape(4, 128, 4, 256).transpose(1, 2, 0, 3).reshape(1, 128, 4096)
+    return pl.pallas_call(
+        finish,
+        out_shape=(
+            jax.ShapeDtypeStruct((1, 128, 4096), BF),
+            jax.ShapeDtypeStruct((1, 128, 4096), BF),
+            jax.ShapeDtypeStruct((1, 128, 1024), F32),
+            jax.ShapeDtypeStruct((1, 1024, 128), F32),
+        ),
+        in_specs=[any_] * 7,
+        out_specs=(any_,) * 4,
+        scratch_shapes=[
+            pltpu.VMEM((2, 4, 128, 1024), BF),
+            pltpu.VMEM((2, 128, 1024), BF),
+            pltpu.VMEM((2, 128, 1024), F32),
+            pltpu.VMEM((2, 1024, 128), F32),
+            pltpu.VMEM((128, 1024), F32),
+            pltpu.VMEM((1024, 128), F32),
+            pltpu.SemaphoreType.DMA((16,)),
+            pltpu.SemaphoreType.DMA((40,)),
+        ],
+        name="finish",
+    )(so, ig, gw, fast_in, fast_out, slow_in, slow_out)
+
+
+def finish(so, ig, gw, fi, fo, si, so_slow, o0, o1, o2, o3, acts, grads, wi, wo, ri, ro, insem, outsem):
+    loads = []
+
+    def load(src, dst):
+        c = pltpu.make_async_copy(src, dst, insem.at[len(loads)])
+        c.start()
+        loads.append(c)
+        return c
+
+    weights = [load(gw, grads), load(fo.at[0], wo.at[0]), load(so_slow.at[0], wo.at[1]),
+               load(fi.at[0], wi.at[0]), load(si.at[0], wi.at[1])]
+    pieces = [[load(t.at[x], acts.at[k, x]) for x in range(4)] for k, t in enumerate((so, ig))]
+    stores = []
+
+    def store(src, dst):
+        c = pltpu.make_async_copy(src, dst, outsem.at[len(stores)])
+        c.start()
+        stores.append(c)
+
+    for k, out in enumerate((o0, o1)):
+        for x in range(4):
+            pieces[k][x].wait()
+            for zz in range(4):
+                at = zz * 1024 + x * 256
+                store(acts.at[k, x, :, zz * 256:(zz + 1) * 256], out.at[0, :, at:at + 256])
 
     def synced(fast, slow, grad):
-        fresh = fast - RATE * grad
-        return slow + MIX * (fresh - slow)
-
-    grad_in = gw[0].astype(F32)
-    grad_out = gw[1].astype(F32).T
-    return (
-        whole(so), whole(ig),
-        synced(fast_in, slow_in, grad_in[None]),
-        synced(fast_out, slow_out, grad_out[None]),
-    )
+        return slow + MIX * ((fast - RATE * grad) - slow)
+
+    for c in weights[:3]:
+        c.wait()
+    ro[...] = synced(wo[0], wo[1], grads[1].astype(F32).T)
+    store(ro, o3.at[0])
+    for c in weights[3:]:
+        c.wait()
+    ri[...] = synced(wi[0], wi[1], grads[0].astype(F32))
+    store(ri, o2.at[0])
+    for c in stores:
+        c.wait()
 
 
 def solution(mesh):

time: 254 us -> 204 us (0.80)
  Pallas kernels: 236 us -> 203 us
  local copies, waits for them, and re-layouts: 11.6 us -> 0 us
  other arithmetic: 3.42 us -> 0 us
    pallas_call x1, Pallas kernels: 236 us -> 200 us  [shards(): pl.pallas_call(relay, out_shape=(jax.ShapeDtypeStruct((4, 128, 1024), BF)...]
    reshape x4 -> x0, local copies, waits for them, and re-layouts: 4.74 us -> none  [whole(): pieces.reshape(4, 128, 4, 256).transpose(1, 2, 0, 3).reshape(1, 128, 4096)]
    unnamed x13 -> x0, local copies, waits for them, and re-layouts: 4.11 us -> none
    pallas_call x0 -> x1, Pallas kernels: none -> 3.94 us  [shards(): pl.pallas_call(finish, out_shape=(jax.ShapeDtypeStruct((1, 128, 4096), BF...]
    add x2 -> x0, other arithmetic: 3.42 us -> none  [synced(): return slow + MIX * (fresh - slow)]
    transpose x2 -> x0, local copies, waits for them, and re-layouts: 2.71 us -> none  [whole(): pieces.reshape(4, 128, 4, 256).transpose(1, 2, 0, 3).reshape(1, 128, 4096)]
where the time goes in v2:
time: 204 us
  Pallas kernels  203 us (100%)
    pallas_call x1, Pallas kernels, shards(): pl.pallas_call(relay, out_shape=(jax.ShapeDtypeStruct((4, 128, 1024), BF)...  200 us

profile of v2, /device:TPU:0, one launch (start us, length us, event | category | flops | bytes accessed | tf_op | source)
XLA Modules:
  0.0 204.1 jit_solution(9027153387304559501)
XLA Ops:
  0.6 199.5 %relay.1 = (bf16[4,128,1024]{2,1,0:T(8,128)(2,1)}, bf16[4,128,1024]{2,1,0:T(8,128)(2,1)}, bf16[2,128,1024]{2,1,0:T(8,128)(2,1)}) custom-call(bf16[128,4096]{1,0:T(8,128)(2,1)} %hid_hbm.1, bf16[128,4096]{1,0:T(8,128)(2,1)} %cot_hbm.1, f32[1,128,1024]{2,1,0:T(8,128)} %fi.1, f32[1,1024,128]{2,1,0:T(8,128)} %fo.1), custom_call_target="tpu_custom_call" | custom-call | tf_op jit(solution)/shard_map/relay/pallas_call | solution.py:581
  200.1 3.9 %finish.1 = (bf16[1,128,4096]{2,1,0:T(8,128)(2,1)}, bf16[1,128,4096]{2,1,0:T(8,128)(2,1)}, f32[1,128,1024]{2,1,0:T(8,128)}, f32[1,1024,128]{2,1,0:T(8,128)}) custom-call(bf16[4,128,1024]{2,1,0:T(8,128)(2,1)} %get-tuple-element.7.so, bf16[4,128,1024]{2,1,0:T(8,128)(2,1)} %get-tuple-element.8.ig, bf16[2,128,1024]{2,1,0:T(8,128)(2,1)} %get-tuple-element.9.gw, ...), custom_call_target="tpu_custom_call" | custom-call | tf_op jit(solution)/shard_map/finish/pallas_call | solution.py:623

commit v3 on v2

--- a/solution.py
+++ b/solution.py
@@ -102,11 +102,9 @@
     mates = sem("r", 8)
 
     def share():
-        loads[0].wait()
-        own[0] = quarters(fin[...] * in_scale)
-        loads[1].wait()
-        own[1] = quarters((fout[...] * out_scale).T)
-        for c in range(2):
+        for c, value in ((0, lambda: fin[...] * in_scale), (1, lambda: (fout[...] * out_scale).T)):
+            loads[c].wait()
+            own[c] = quarters(value())
             push(own.at[c, 1 - yh], W.at[s, c, z, yl, 1 - yh], mates + core, ((1 - yh) * 2 + c, f))
         push(own.at[:, yh], W.at[s, :, z, yl, yh], mates + 2, partner)
         W[s, 0, z, yl, yh] = own[0, yh]
@@ -134,32 +132,36 @@
         return base
 
     def ag_ring(item, half, q, to_plus, to_minus, level):
-        base = sem("r", 8)
+        base = sem("r", 10)
         qp, qm, qo = (q + 1) % 4, (q + 3) % 4, (q + 2) % 4
-        push(item(q), item(q), base + 0, to_plus)
-        push(item(q), item(q), base + 1, to_minus)
-        yield
-        got(item(qm), base + 0)
-        push(half(qm, 0), half(qm, 0), base + 2, to_plus)
-        got(item(qp), base + 1)
-        push(half(qp, 1), half(qp, 1), base + 3, to_minus)
-        push(item(qm), item(qm), base + 4, partner)
-        push(item(qp), item(qp), base + 5, partner)
-        yield
-        got(half(qo, 0), base + 2)
-        push(half(qo, 0), half(qo, 0), base + 6, partner)
-        got(half(qo, 1), base + 3)
-        push(half(qo, 1), half(qo, 1), base + 7, partner)
+        push(half(q, 0), half(q, 0), base + 0, to_plus)
+        push(half(q, 1), half(q, 1), base + 1, to_minus)
+        push(half(q, 1), half(q, 1), base + 2, to_plus)
+        push(half(q, 0), half(q, 0), base + 3, to_minus)
+        yield
+        got(half(qm, 0), base + 0)
+        push(half(qm, 0), half(qm, 0), base + 4, to_plus)
+        got(half(qp, 1), base + 1)
+        push(half(qp, 1), half(qp, 1), base + 5, to_minus)
+        got(half(qm, 1), base + 2)
+        push(item(qm), item(qm), base + 6, partner)
+        got(half(qp, 0), base + 3)
+        push(item(qp), item(qp), base + 7, partner)
+        yield
+        got(half(qo, 0), base + 4)
+        push(half(qo, 0), half(qo, 0), base + 8, partner)
+        got(half(qo, 1), base + 5)
+        push(half(qo, 1), half(qo, 1), base + 9, partner)
         pending.append((level, lambda: twin(item, half, q, base)))
 
     pending = []
 
     def twin(item, half, q, base):
         qp, qm, qo = (q + 1) % 4, (q + 3) % 4, (q + 2) % 4
-        got(item(qm, other), base + 4)
-        got(item(qp, other), base + 5)
-        got(half(qo, 0, other), base + 6)
-        got(half(qo, 1, other), base + 7)
+        got(item(qm, other), base + 6)
+        got(item(qp, other), base + 7)
+        got(half(qo, 0, other), base + 8)
+        got(half(qo, 1, other), base + 9)
 
     def settle(level):
         for entry in list(pending):
@@ -229,13 +231,13 @@
             right = W[l, k, :, :, :, :, :, pl.ds(c, NT)].reshape(1024, NT)
             stg[step, :, :, pl.ds(c, NT)] = dot_nn(left, right).astype(BF).reshape(4, 32, NT)
             return carry
-        lax.fori_loop(0, LAT // NT, body, 0)
+        lax.fori_loop(0, LAT // NT, body, 0, unroll=True)
 
     def scatter(step):
         base = sem("r", 4)
-        land[step, x] = stg[step, x]
         for d in (2, 1, 3):
             push(stg.at[step, (x + d) % 4], land.at[step, x], base + d, xdev(d))
+        land[step, x] = stg[step, x]
         return base
 
     def summed(step, base):
@@ -284,11 +286,12 @@
 
     parts_due = []
 
-    def emit_next():
-        if parts_due:
+    def emit_next(last=False):
+        counters["w"] += 1
+        if parts_due and (last or counters["w"] > EMIT_FROM):
             parts_due.pop(0)()
 
-    counters["l"] = 0
+    counters["l"] = counters["w"] = 0
     locals_, emitted = [], []
 
     def finish_emit():
@@ -323,10 +326,10 @@
             total = total + land[l, xx].astype(F32)
         r = lax.rsqrt(join_lanes(total[:, LAT:]) * (1.0 / D) + EPS)
         v = total[:, :LAT] * r
+        act[l, x] = (v / (1.0 + jnp.exp(-v))).astype(BF)
+        base = broadcast(act, l)
         pre[l] = v
         rinv[l] = jnp.broadcast_to(r, (32, EXT))
-        act[l, x] = (v / (1.0 + jnp.exp(-v))).astype(BF)
-        base = broadcast(act, l)
         emit_next()
         yield
         collect(act, l, base)
@@ -338,7 +341,7 @@
             old = h[l, :, :, pl.ds(c, NT)].reshape(128, NT).astype(F32)
             h[l + 1, :, :, pl.ds(c, NT)] = (old + dot_nt(left, right)).astype(BF).reshape(4, 32, NT)
             return carry
-        lax.fori_loop(0, 4, body, 0)
+        lax.fori_loop(0, 4, body, 0, unroll=True)
         emit(h, l + 1, l, so_hbm)
 
     def wgrad(l, kind, left_ref, left_level, right_ref, scale):
@@ -350,14 +353,21 @@
             value = (dot_tn(left, right) * scale).astype(BF)
             G[l, kind, i // 2, i % 2] = value.reshape(2, 2, 32, LAT)
             return carry
-        lax.fori_loop(0, 8, body, 0)
+        lax.fori_loop(0, 8, body, 0, unroll=4)
+
+    begun = {}
+
+    def begin(l):
+        project(g, l + 1, l, 1, 7 - l)
+        begun[l] = scatter(7 - l)
 
     def backward(l):
         step = 7 - l
-        project(g, l + 1, l, 1, step)
-        base = scatter(step)
+        if l not in begun:
+            begin(l)
+        base = begun[l]
         emit_next()
-        if l < 3:
+        if 1 < l + 1 < 4 and l > 0:
             input_grads(l + 1)
         yield
         summed(step, base)
@@ -379,8 +389,8 @@
         left = pgb[l, :, :, :LAT].reshape(128, LAT)
         kap = join_lanes(pgb[l, :, :, LAT:].reshape(128, EXT))
 
-        if l == 0:
-            input_grads(0)
+        if l < 2:
+            input_grads(l)
 
         def body(i, carry):
             c = pl.multiple_of(i * NT, NT)
@@ -389,7 +399,7 @@
             base_h = h[l, :, :, pl.ds(c, NT)].reshape(128, NT).astype(F32)
             g[l, :, :, pl.ds(c, NT)] = (old + dot_nt(left, right) - base_h * kap).astype(BF).reshape(4, 32, NT)
             return carry
-        lax.fori_loop(0, 4, body, 0)
+        lax.fori_loop(0, 4, body, 0, unroll=True)
         emit(g, l, l, ig_hbm)
 
     def input_grads(l):
@@ -539,26 +549,39 @@
         got(h.at[0, (x + 4 - d) % 4], hbase + d)
     for l in range(4):
         need(l)
-        for _ in forward(l):
+        for n, _ in enumerate(forward(l)):
             step(bulk)
-    for d in (1, 3, 2):
-        got(g.at[4, (x + 4 - d) % 4], gbase + d)
+            if l == 3 and n == 1:
+                for d in (1, 3, 2):
+                    got(g.at[4, (x + 4 - d) % 4], gbase + d)
+                begin(3)
     running = []
+
+    def poll(tasks):
+        for task in list(tasks):
+            step(task)
+
+    def launch(l):
+        merge(l)
+        running.append(reduce_round(l))
+        step(running[-1])
+
     for l in (3, 2, 1, 0):
         for n, _ in enumerate(backward(l)):
-            for task in running:
-                step(task)
-            if n == 1 and l < 3:
-                merge(l + 1)
-                running.append(reduce_round(l + 1))
-                step(running[-1])
+            poll(running[:1])
+            if n == 0 and l == 0:
+                launch(1)
+            if n == 1 and l in (2, 1):
+                launch(l + 1)
+        if POLL:
+            poll(running[:POLL])
+    poll(running)
+    launch(0)
     while parts_due:
-        emit_next()
-    for task in running:
-        step(task)
-    merge(0)
-    running.append(reduce_round(0))
-    drain(zipped(running))
+        emit_next(True)
+    remaining = zipped(running)
+    step(remaining)
+    drain(remaining)
     for l, copy in sent_home:
         @pl.when(s != l)
         def _():
@@ -573,7 +596,9 @@
     assert counters["s"] <= SENDS and counters["r"] <= RECVS and counters["l"] <= 8, counters
 
 
-SENDS, RECVS = 352, 480
+SENDS, RECVS = 384, 512
+POLL = 0
+EMIT_FROM = 0
 
 
 def shards(hidden_in, out_grad, fast_in, fast_out, slow_in, slow_out):

time: 204 us -> 195 us (0.956); the launches traced: 204 us -> 191 us
  Pallas kernels: 203 us -> 190 us
    pallas_call x1, Pallas kernels: 200 us -> 186 us  [shards(): pl.pallas_call(relay, out_shape=(jax.ShapeDtypeStruct((4, 128, 1024), BF)...]
where the time goes in v3:
time: 195 us; the launch traced here: 191 us
  Pallas kernels  190 us (97%)
    pallas_call x1, Pallas kernels, shards(): pl.pallas_call(relay, out_shape=(jax.ShapeDtypeStruct((4, 128, 1024), BF)...  186 us
    pallas_call x1, Pallas kernels, shards(): pl.pallas_call(finish, out_shape=(jax.ShapeDtypeStruct((1, 128, 4096), BF...  3.94 us

profile of v3, /device:TPU:0, one launch (start us, length us, event | category | flops | bytes accessed | tf_op | source)
XLA Modules:
  0.0 191.0 jit_solution(827479493404646171)
XLA Ops:
  0.6 186.3 %relay.1 = (bf16[4,128,1024]{2,1,0:T(8,128)(2,1)}, bf16[4,128,1024]{2,1,0:T(8,128)(2,1)}, bf16[2,128,1024]{2,1,0:T(8,128)(2,1)}) custom-call(bf16[128,4096]{1,0:T(8,128)(2,1)} %hid_hbm.1, bf16[128,4096]{1,0:T(8,128)(2,1)} %cot_hbm.1, f32[1,128,1024]{2,1,0:T(8,128)} %fi.1, f32[1,1024,128]{2,1,0:T(8,128)} %fo.1), custom_call_target="tpu_custom_call" | custom-call | tf_op jit(solution)/shard_map/relay/pallas_call | solution.py:606
  186.9 3.9 %finish.1 = (bf16[1,128,4096]{2,1,0:T(8,128)(2,1)}, bf16[1,128,4096]{2,1,0:T(8,128)(2,1)}, f32[1,128,1024]{2,1,0:T(8,128)}, f32[1,1024,128]{2,1,0:T(8,128)}) custom-call(bf16[4,128,1024]{2,1,0:T(8,128)(2,1)} %get-tuple-element.7.so, bf16[4,128,1024]{2,1,0:T(8,128)(2,1)} %get-tuple-element.8.ig, bf16[2,128,1024]{2,1,0:T(8,128)(2,1)} %get-tuple-element.9.gw, ...), custom_call_target="tpu_custom_call" | custom-call | tf_op jit(solution)/shard_map/finish/pallas_call | solution.py:648

commit v4 on v3

--- a/solution.py
+++ b/solution.py
@@ -31,7 +31,7 @@
 def relay(
     hid_hbm, cot_hbm, fin_hbm, fout_hbm,
     so_hbm, ig_hbm, gw_ref,
-    fin, fout, hid, cot, stage0, own, W, G, Gx, h, g, stg, land, act, pgb, pre, rinv,
+    fin, fout, hid, cot, stage0, own, W, G, Gx, h, g, stgs, lands, stg, land, act, pg0, pg1, pre, rinv,
     z1, z2, za, zb, gw,
     in_sem, s_send, s_recv,
 ):
@@ -223,36 +223,53 @@
 
     NT = 256
 
-    def project(source, level, l, k, step):
+    HALF = LAT // 2
+
+    def slots(step, n, sums):
+        if sums and n == 0:
+            return stgs.at[step], lands.at[step]
+        at = 2 * step + n
+        return stg.at[at], land.at[at]
+
+    def project(source, level, l, k, step, sums):
         left = source[level].reshape(128, 1024)
-
-        def body(i, carry):
-            c = pl.multiple_of(i * NT, NT)
-            right = W[l, k, :, :, :, :, :, pl.ds(c, NT)].reshape(1024, NT)
-            stg[step, :, :, pl.ds(c, NT)] = dot_nn(left, right).astype(BF).reshape(4, 32, NT)
-            return carry
-        lax.fori_loop(0, LAT // NT, body, 0, unroll=True)
-
-    def scatter(step):
-        base = sem("r", 4)
+        base = sem("r", 8)
+        for n in range(2):
+            out, landing = slots(step, n, sums)
+            for c in range(0, HALF, NT):
+                right = W[l, k, :, :, :, :, :, n * HALF + c:n * HALF + c + NT].reshape(1024, NT)
+                out[:, :, c:c + NT] = dot_nn(left, right).astype(BF).reshape(4, 32, NT)
+            for d in (2, 1, 3):
+                push(out.at[(x + d) % 4], landing.at[x], base + 4 * n + d, xdev(d))
+            landing[x] = out[x]
+        return base
+
+    def summed(step, n, base, sums):
+        landing = slots(step, n, sums)[1]
+        for d in (1, 3, 2):
+            got(landing.at[(x + 4 - d) % 4], base + 4 * n + d)
+        total = landing[0].astype(F32)
+        for xx in range(1, 4):
+            total = total + landing[xx].astype(F32)
+        return total
+
+    def broadcast(buf, n, base):
         for d in (2, 1, 3):
-            push(stg.at[step, (x + d) % 4], land.at[step, x], base + d, xdev(d))
-        land[step, x] = stg[step, x]
-        return base
-
-    def summed(step, base):
-        for d in (1, 3, 2):
-            got(land.at[step, (x + 4 - d) % 4], base + d)
-
-    def broadcast(buf, l):
-        base = sem("r", 4)
-        for d in (2, 1, 3):
-            push(buf.at[l, x], buf.at[l, x], base + d, xdev(d))
-        return base
-
-    def collect(buf, l, base):
-        for d in (1, 3, 2):
-            got(buf.at[l, (x + 4 - d) % 4], base + d)
+            push(buf.at[x], buf.at[x], base + 4 * n + d, xdev(d))
+
+    def collect(bufs, base):
+        for n in range(2):
+            for d in (1, 3, 2):
+                got(bufs[n].at[(x + 4 - d) % 4], base + 4 * n + d)
+
+    def full(bufs):
+        return jnp.concatenate([b[:, :, :HALF].reshape(128, HALF) for b in bufs], axis=-1)
+
+    def acts(l):
+        return act.at[l, 0], act.at[l, 1]
+
+    def grads(l):
+        return pg0.at[l], pg1.at[l]
 
     def emit(source, level, l, out_ref):
         base = sem("r", 16)
@@ -313,27 +330,28 @@
                             got(out_ref.at[xx, pl.ds(pl.multiple_of(ss * 32, 32), 32)], base + ss * 4 + xx)
 
     def forward(l):
-        project(h, l, l, 0, l)
         wide = h[l].reshape(128, 1024).astype(F32)
         ss = jnp.sum(wide * wide, axis=-1, keepdims=True)
-        stg[l, :, :, LAT:] = split_lanes(ss).reshape(4, 32, EXT)
-        base = scatter(l)
+        stgs[l, :, :, HALF:] = split_lanes(ss).reshape(4, 32, EXT)
+        base = project(h, l, l, 0, l, True)
         emit_next()
         yield
-        summed(l, base)
-        total = land[l, 0].astype(F32)
-        for xx in range(1, 4):
-            total = total + land[l, xx].astype(F32)
-        r = lax.rsqrt(join_lanes(total[:, LAT:]) * (1.0 / D) + EPS)
-        v = total[:, :LAT] * r
-        act[l, x] = (v / (1.0 + jnp.exp(-v))).astype(BF)
-        base = broadcast(act, l)
-        pre[l] = v
+        away = sem("r", 8)
+        r = None
+        for n in range(2):
+            total = summed(l, n, base, True)
+            if n == 0:
+                r = lax.rsqrt(join_lanes(total[:, HALF:]) * (1.0 / D) + EPS)
+                total = total[:, :HALF]
+            v = total * r
+            act[l, n, x] = (v / (1.0 + jnp.exp(-v))).astype(BF)
+            broadcast(act.at[l, n], n, away)
+            pre[l, :, n * HALF:(n + 1) * HALF] = v
         rinv[l] = jnp.broadcast_to(r, (32, EXT))
         emit_next()
         yield
-        collect(act, l, base)
-        left = act[l].reshape(128, 1024)
+        collect(acts(l), away)
+        left = full(acts(l))
 
         def body(i, carry):
             c = pl.multiple_of(i * NT, NT)
@@ -345,7 +363,7 @@
         emit(h, l + 1, l, so_hbm)
 
     def wgrad(l, kind, left_ref, left_level, right_ref, scale):
-        right = right_ref[l, :, :, :LAT].reshape(128, LAT)
+        right = full(right_ref(l))
 
         def body(i, carry):
             c = pl.multiple_of(i * 128, 128)
@@ -358,8 +376,7 @@
     begun = {}
 
     def begin(l):
-        project(g, l + 1, l, 1, 7 - l)
-        begun[l] = scatter(7 - l)
+        begun[l] = project(g, l + 1, l, 1, 7 - l, False)
 
     def backward(l):
         step = 7 - l
@@ -370,27 +387,29 @@
         if 1 < l + 1 < 4 and l > 0:
             input_grads(l + 1)
         yield
-        summed(step, base)
-        total = land[step, 0, :, :LAT].astype(F32)
-        for xx in range(1, 4):
-            total = total + land[step, xx, :, :LAT].astype(F32)
-        v = pre[l]
+        away = sem("r", 8)
         r = rinv[l][:, :1]
-        sg = 1.0 / (1.0 + jnp.exp(-v))
-        scaled = (r * (total * sg * (1.0 + v * (1.0 - sg)))).astype(BF)
-        kappa = r * jnp.sum(scaled.astype(F32) * v, axis=-1, keepdims=True) * (1.0 / D)
-        pgb[l, x, :, :LAT] = scaled
-        pgb[l, x, :, LAT:] = split_lanes(kappa)
-        base = broadcast(pgb, l)
+        dots = None
+        for n in range(2):
+            total = summed(step, n, base, False)
+            v = pre[l, :, n * HALF:(n + 1) * HALF]
+            sg = 1.0 / (1.0 + jnp.exp(-v))
+            scaled = (r * (total * sg * (1.0 + v * (1.0 - sg)))).astype(BF)
+            term = jnp.sum(scaled.astype(F32) * v, axis=-1, keepdims=True)
+            dots = term if n == 0 else dots + term
+            part = grads(l)[n]
+            part[x, :, :HALF] = scaled
+            if n:
+                part[x, :, HALF:] = split_lanes(r * dots * (1.0 / D))
+            broadcast(part, n, away)
         emit_next()
-        wgrad(l, 1, g, l + 1, act, out_scale)
-        yield
-        collect(pgb, l, base)
-        left = pgb[l, :, :, :LAT].reshape(128, LAT)
-        kap = join_lanes(pgb[l, :, :, LAT:].reshape(128, EXT))
-
+        wgrad(l, 1, g, l + 1, acts, out_scale)
+        yield
+        collect(grads(l), away)
         if l < 2:
             input_grads(l)
+        left = full(grads(l))
+        kap = join_lanes(pg1[l, :, :, HALF:].reshape(128, EXT))
 
         def body(i, carry):
             c = pl.multiple_of(i * NT, NT)
@@ -403,7 +422,7 @@
         emit(g, l, l, ig_hbm)
 
     def input_grads(l):
-        wgrad(l, 0, h, l, pgb, in_scale)
+        wgrad(l, 0, h, l, grads, in_scale)
         gx_base[l] = sem("r")
         push(G.at[l, other], Gx.at[l], gx_base[l], partner)
 
@@ -624,10 +643,13 @@
             pltpu.VMEM((4, 4, 2, 2, 2, 32, 1024), BF),
             pltpu.VMEM((5, 4, 32, 1024), BF),
             pltpu.VMEM((5, 4, 32, 1024), BF),
-            pltpu.VMEM((8, 4, 32, 1024 + EXT), BF),
-            pltpu.VMEM((8, 4, 32, 1024 + EXT), BF),
-            pltpu.VMEM((4, 4, 32, 1024), BF),
-            pltpu.VMEM((4, 4, 32, 1024 + EXT), BF),
+            pltpu.VMEM((4, 4, 32, 512 + EXT), BF),
+            pltpu.VMEM((4, 4, 32, 512 + EXT), BF),
+            pltpu.VMEM((16, 4, 32, 512), BF),
+            pltpu.VMEM((16, 4, 32, 512), BF),
+            pltpu.VMEM((4, 2, 4, 32, 512), BF),
+            pltpu.VMEM((4, 4, 32, 512), BF),
+            pltpu.VMEM((4, 4, 32, 512 + EXT), BF),
             pltpu.VMEM((4, 32, 1024), F32),
             pltpu.VMEM((4, 32, EXT), F32),
             pltpu.VMEM((4, 2, 2, 2, 32, 1024), BF),

time: 195 us -> 195 us (level); the launches traced: 191 us -> 195 us
  Pallas kernels: 190 us -> 194 us
    pallas_call x1, Pallas kernels: 186 us -> 190 us  [shards(): pl.pallas_call(relay, out_shape=(jax.ShapeDtypeStruct((4, 128, 1024), BF)...]
where the time goes in v4:
time: 195 us
  Pallas kernels  194 us (99%)
    pallas_call x1, Pallas kernels, shards(): pl.pallas_call(relay, out_shape=(jax.ShapeDtypeStruct((4, 128, 1024), BF)...  190 us
    pallas_call x1, Pallas kernels, shards(): pl.pallas_call(finish, out_shape=(jax.ShapeDtypeStruct((1, 128, 4096), BF...  3.94 us

profile of v4, /device:TPU:0, one launch (start us, length us, event | category | flops | bytes accessed | tf_op | source)
XLA Modules:
  0.0 194.7 jit_solution(6016225035614664977)
XLA Ops:
  0.6 189.9 %relay.1 = (bf16[4,128,1024]{2,1,0:T(8,128)(2,1)}, bf16[4,128,1024]{2,1,0:T(8,128)(2,1)}, bf16[2,128,1024]{2,1,0:T(8,128)(2,1)}) custom-call(bf16[128,4096]{1,0:T(8,128)(2,1)} %hid_hbm.1, bf16[128,4096]{1,0:T(8,128)(2,1)} %cot_hbm.1, f32[1,128,1024]{2,1,0:T(8,128)} %fi.1, f32[1,1024,128]{2,1,0:T(8,128)} %fo.1), custom_call_target="tpu_custom_call" | custom-call | tf_op jit(solution)/shard_map/relay/pallas_call | solution.py:625
  190.6 3.9 %finish.1 = (bf16[1,128,4096]{2,1,0:T(8,128)(2,1)}, bf16[1,128,4096]{2,1,0:T(8,128)(2,1)}, f32[1,128,1024]{2,1,0:T(8,128)}, f32[1,1024,128]{2,1,0:T(8,128)}) custom-call(bf16[4,128,1024]{2,1,0:T(8,128)(2,1)} %get-tuple-element.7.so, bf16[4,128,1024]{2,1,0:T(8,128)(2,1)} %get-tuple-element.8.ig, bf16[2,128,1024]{2,1,0:T(8,128)(2,1)} %get-tuple-element.9.gw, ...), custom_call_target="tpu_custom_call" | custom-call | tf_op jit(solution)/shard_map/finish/pallas_call | solution.py:670
